TPU v7x, 16 devices: a whole 2x2x2 slice. The times are simulated.
16 devices in a mesh: data: 4 (over z, y), sp: 4 (over x, core).
Axes of the slice: x: 2, y: 2, z: 2, core: 2. Of those that a mesh axis runs over, the one named last changes fastest.
Arguments:
- latents: bfloat16 [4, 16, 256, 384], P('data', 'sp'), parts along dimension 0
- norms: float32 [4, 4, 384], replicated
- w_qkv: bfloat16 [4, 384, 3, 6, 64], replicated
- w_out: bfloat16 [4, 6, 64, 384], replicated
- w_up: bfloat16 [4, 384, 1536], replicated
- w_down: bfloat16 [4, 1536, 384], replicated
Outputs:
- output: bfloat16 [4, 16, 256, 384], P('data', None, 'sp'), parts along dimension 0
There are 4 independent parts. A program takes and returns all parts, laid end to end along the dimension named above; an argument that names none is the same for every part.
All inputs are finite; a program needn't handle non-finite values.
Results may differ from a plain program's by a relative error of at most 0.0159482.
Values are sent between devices in bfloat16 or wider.
A program may use at most 1 GiB of HBM per device.

v0:
```python
import math
import jax
import jax.numpy as jnp
from jax import lax
from jax.sharding import PartitionSpec as P

EPS = 1e-6
SPATIAL = (2, 'btqhe,btkhe->bthqk', 'bthqk,btkhe->btqhe')
TEMPORAL = (1, 'bqshe,bkshe->bshqk', 'bshqk,bkshe->bqshe')


def layer_norm(tokens, norm_gain, norm_shift):
    tokens_f32 = tokens.astype(jnp.float32)
    row_mean = jnp.mean(tokens_f32, axis=-1, keepdims=True)
    centered = tokens_f32 - row_mean
    variance = jnp.mean(jnp.square(centered), axis=-1, keepdims=True)
    return (centered * lax.rsqrt(variance + EPS) * norm_gain + norm_shift).astype(jnp.bfloat16)


def attention(query_rows, key_rows, value_rows, layout):
    seq_axis, score_form, mix_form = layout
    seq_len = query_rows.shape[seq_axis]
    q_block = math.gcd(seq_len, 128)
    logit_scale = query_rows.shape[-1] ** -0.5

    def attend_block(block_idx, attn_out):
        q_start = block_idx * q_block
        q_part = lax.dynamic_slice_in_dim(query_rows, q_start, q_block, axis=seq_axis)
        logits = jnp.einsum(score_form, q_part, key_rows, preferred_element_type=jnp.float32) * logit_scale
        attn_probs = jax.nn.softmax(logits, axis=-1).astype(jnp.bfloat16)
        block_out = jnp.einsum(mix_form, attn_probs, value_rows, preferred_element_type=jnp.float32).astype(jnp.bfloat16)
        return lax.dynamic_update_slice_in_dim(attn_out, block_out, q_start, axis=seq_axis)

    return lax.fori_loop(0, seq_len // q_block, attend_block, jnp.zeros_like(query_rows))


def project_heads(normed, head_weight):
    return jnp.einsum('btsd,dhe->btshe', normed, head_weight, preferred_element_type=jnp.float32).astype(jnp.bfloat16)


def transformer_block(tokens, norm_rows, qkv_weight, out_weight, up_weight, down_weight, layout):
    normed = layer_norm(tokens, norm_rows[0], norm_rows[1])
    mixed_heads = attention(project_heads(normed, qkv_weight[:, 0]), project_heads(normed, qkv_weight[:, 1]), project_heads(normed, qkv_weight[:, 2]), layout)
    attn_proj = jnp.einsum('btshe,hed->btsd', mixed_heads, out_weight, preferred_element_type=jnp.float32)
    residual = (tokens.astype(jnp.float32) + attn_proj).astype(jnp.bfloat16)
    normed_mlp = layer_norm(residual, norm_rows[2], norm_rows[3])
    up_proj = jnp.einsum('btsd,df->btsf', normed_mlp, up_weight, preferred_element_type=jnp.float32)
    hidden = jax.nn.gelu(up_proj, approximate=True).astype(jnp.bfloat16)
    down_proj = jnp.einsum('btsf,fd->btsd', hidden, down_weight, preferred_element_type=jnp.float32)
    return (residual.astype(jnp.float32) + down_proj).astype(jnp.bfloat16)


def solution(mesh):
    def local_stack(latents, norms, w_qkv, w_out, w_up, w_down):
        tokens = latents
        for layer_idx in range(w_qkv.shape[0]):
            if layer_idx % 2 == 1:
                tokens = lax.all_to_all(tokens, 'sp', 2, 1, tiled=True)
                layout = TEMPORAL
            else:
                if layer_idx > 0:
                    tokens = lax.all_to_all(tokens, 'sp', 1, 2, tiled=True)
                layout = SPATIAL
            tokens = transformer_block(tokens, norms[layer_idx], w_qkv[layer_idx], w_out[layer_idx], w_up[layer_idx], w_down[layer_idx], layout)
        return tokens

    replicated = P()
    return jax.shard_map(local_stack, mesh=mesh, in_specs=(P('data', 'sp', None, None), replicated, replicated, replicated, replicated, replicated), out_specs=P('data', None, 'sp', None), check_vma=False)
```

profile of v0, /device:TPU:0, one launch (start us, length us, event | category | flops | bytes accessed | tf_op | source)
XLA Modules:
  0.0 188.2 jit_solution(15494382126528505006)
XLA Ops:
  0.0 3.7 %slice_bitcast_fusion = (bf16[384,3,6,64]{0,3,2,1:T(8,128)(2,1)}, bf16[384,3,6,64]{0,3,2,1:T(8,128)(2,1)}, bf16[384,3,6,64]{0,3,2,1:T(8,128)(2,1)S(1)}, bf16[384,3,6,64]{0,3,2,1:T(8,128)(2,1)}) fusion(bf16[4,384,3,6,64]{1,4,3,2,0:T(8,128)(2,1)} %param.12), kind=kLoop, calls=%fused_computation.213 | loop fusion | bytes 7077888 | tf_op jit(solution)/shard_map/squeeze | solution.py:64
  4.5 1.7 fusion.154
  6.2 1.7 fusion.155
  7.8 1.7 fusion.156
  10.5 21.0 %while.16 = (s32[]{:T(128)}, bf16[1,4,256,6,64]{2,4,3,1,0:T(8,128)(2,1)}, bf16[1,4,256,6,64]{2,4,3,1,0:T(8,128)(2,1)}, bf16[1,4,256,6,64]{2,4,3,1,0:T(8,128)(2,1...) while((s32[]{:T(128)}, ...), condition=%wide.region_5.0_spmd, body=%wide.region_2.0_spmd.sunk | while | flops 208604672 | bytes 14971035 | solution.py:34
  10.8 1.9 fusion.296
  13.7 7.4 %fusion.298 = bf16[1,4,256,6,64]{2,4,3,1,0:T(8,128)(2,1)} fusion(bf16[1,4,256,6,64]{2,4,3,1,0:T(8,128)(2,1)} %get-tuple-element.355, s32[]{:T(128)S(6)} %select_n.24, f32[4,6,128]{2,1,0:T(8,128)S(1)} %fusion.297, bf16[1,4,256,6,64]{2,4,3,1,0:T(8,128)(2,1)} %get-tuple-element.367, f32[4,6,128,256]{3,2,1,0:T(8,128)S(1)} %fusion.296), kind=kOutput, calls=%fused_computation.9.clone.1 | convolution fusion | flops 104795392 | bytes 7487492 | tf_op jit(solution)/shard_map/while/body/eval_jaxpr/bthqk,btkhe->btqhe/dot_general | solution.py:31
  21.1 1.9 fusion.296
  24.1 7.4 %fusion.298 = bf16[1,4,256,6,64]{2,4,3,1,0:T(8,128)(2,1)} fusion(bf16[1,4,256,6,64]{2,4,3,1,0:T(8,128)(2,1)} %get-tuple-element.355, s32[]{:T(128)S(6)} %select_n.24, f32[4,6,128]{2,1,0:T(8,128)S(1)} %fusion.297, bf16[1,4,256,6,64]{2,4,3,1,0:T(8,128)(2,1)} %get-tuple-element.367, f32[4,6,128,256]{3,2,1,0:T(8,128)S(1)} %fusion.296), kind=kOutput, calls=%fused_computation.9.clone.1 | convolution fusion | flops 104795392 | bytes 7487492 | tf_op jit(solution)/shard_map/while/body/eval_jaxpr/bthqk,btkhe->btqhe/dot_general | solution.py:31
  31.5 2.3 %convert_reduce_fusion.3 = (f32[4,256]{1,0:T(4,128)S(1)}, bf16[1,4,256,384]{3,2,1,0:T(8,128)(2,1)S(1)}) fusion(bf16[4,6,64,384]{3,2,1,0:T(8,128)(2,1)} %param.13, bf16[1,4,256,6,64]{2,4,3,1,0:T(8,128)(2,1)} %get-tuple-element.229, bf16[1,4,256,384]{3,2,1,0:T(8,128)(2,1)} %param.10), kind=kOutput, calls=%fused_computation.95 | convolution fusion | flops 303954944 | bytes 2658304 | tf_op jit(solution)/shard_map/btshe,hed->btsd/dot_general | solution.py:44
  34.2 5.2 %fusion.121 = bf16[1,4,256,384]{3,2,1,0:T(8,128)(2,1)S(1)} fusion(bf16[1,4,256,384]{3,2,1,0:T(8,128)(2,1)S(1)} %get-tuple-element.276, bf16[4,1536,384]{2,1,0:T(8,128)(2,1)} %param.15, bf16[4,384,1536]{2,1,0:T(8,128)(2,1)} %param.14, f32[384]{0:T(512)S(1)} %get-tuple-element.242, f32[384]{0:T(512)S(1)} %get-tuple-element.243, ...), kind=kOutput, calls=%fused_computation.142 | convolution fusion | flops 2433613824 | bytes 4730880 | tf_op jit(solution)/shard_map/btsf,fd->btsd/dot_general | solution.py:49
  40.1 16.2 %all_to_all.12 = bf16[1,4,256,384]{3,1,0,2:T(4,128)(2,1)S(1)} all-to-all(bf16[1,4,256,384]{3,1,0,2:T(4,128)(2,1)S(1)} %copy.66), channel_id=1, replica_groups=mesh['data'=4,'sp'=4] {'sp'}, dimensions={2} | all-to-all | bytes 1572864 | tf_op jit(solution)/shard_map/all_to_all | solution.py:58
  61.5 3.5 %fusion.137 = f32[64,6,16,16]{2,3,1,0:T(8,128)S(1)} fusion(bf16[16,64,6,64]{3,1,2,0:T(8,128)(2,1)S(1)} %convolution_convert_fusion.5, bf16[16,64,6,64]{3,1,2,0:T(8,128)(2,1)S(1)} %convolution_convert_fusion.6), kind=kOutput, calls=%fused_computation.164 | convolution fusion | flops 12582912 | bytes 1966080 | tf_op jit(solution)/shard_map/while/body/eval_jaxpr/bqshe,bkshe->bshqk/dot_general | solution.py:29
  65.1 12.7 %fusion.267 = (f32[64,6,16]{2,1,0:T(8,128)S(1)}, f32[64,6,16,16]{2,3,1,0:T(8,128)S(1)}) fusion(f32[64,6,16,16]{2,3,1,0:T(8,128)S(1)} %fusion.137), kind=kOutput, calls=%fused_computation.311 | output fusion | flops 393231 | bytes 811008 | tf_op jit(solution)/shard_map/while/body/eval_jaxpr/sub | solution.py:30
  77.7 1.8 fusion.144
  79.6 1.9 fusion.127
  82.2 6.1 %fusion.162 = bf16[1,16,64,384]{3,2,0,1:T(8,128)(2,1)} fusion(bf16[16,64,384]{2,1,0:T(8,128)(2,1)S(1)} %fusion.127, bf16[4,1536,384]{2,1,0:T(8,128)(2,1)} %param.15, bf16[4,384,1536]{2,1,0:T(8,128)(2,1)} %param.14, f32[384]{0:T(512)S(1)} %get-tuple-element.238, f32[384]{0:T(512)S(1)} %get-tuple-element.239, f32[16,64]{1,0:T(8,128)S(1)} %add_rsqrt_fusion.3, ...), kind=kOutput, calls=%fused_computation.193 | convolution fusion | flops 2433613824 | bytes 4739072 | tf_op jit(solution)/shard_map/btsf,fd->btsd/dot_general | solution.py:49
  88.3 3.7 %all-to-all-start.1 = ((bf16[1,16,64,384]{3,2,0,1:T(8,128)(2,1)}), bf16[1,16,64,384]{3,2,0,1:T(8,128)(2,1)S(1)}, u32[]{:S(2)}, u32[]{:S(2)}) async-start(bf16[1,16,64,384]{3,2,0,1:T(8,128)(2,1)} %fusion.162), calls=%async_computation.1 | async-start | bytes 1572864 | tf_op jit(solution)/shard_map/all_to_all | solution.py:62
  92.0 11.4 %all-to-all-done.1 = bf16[1,16,64,384]{3,2,0,1:T(8,128)(2,1)S(1)} async-done(((bf16[1,16,64,384]{3,2,0,1:T(8,128)(2,1)}), bf16[1,16,64,384]{3,2,0,1:T(8,128)(2,1)S(1)}, u32[]{:S(2)}, u32[]{:S(2)}) %all-to-all-start.1) | async-done | bytes 786464 | tf_op jit(solution)/shard_map/all_to_all | solution.py:62
  112.1 20.9 %while.17 = (s32[]{:T(128)}, bf16[1,4,256,6,64]{2,4,3,1,0:T(8,128)(2,1)}, bf16[1,4,256,6,64]{2,4,3,1,0:T(8,128)(2,1)}, bf16[1,4,256,6,64]{2,4,3,1,0:T(8,128)(2,1...) while((s32[]{:T(128)}, ...), condition=%wide.region_19.20_spmd, body=%wide.region_16.19_spmd.sunk | while | flops 208604672 | bytes 14971035 | solution.py:34
  112.1 1.9 fusion.303
  115.1 7.4 %fusion.305 = bf16[1,4,256,6,64]{2,4,3,1,0:T(8,128)(2,1)} fusion(bf16[1,4,256,6,64]{2,4,3,1,0:T(8,128)(2,1)} %get-tuple-element.382, s32[]{:T(128)S(6)} %select_n.25, f32[4,6,128]{2,1,0:T(8,128)S(1)} %fusion.304, bf16[1,4,256,6,64]{2,4,3,1,0:T(8,128)(2,1)} %get-tuple-element.394, f32[4,6,128,256]{3,2,1,0:T(8,128)S(1)} %fusion.303), kind=kOutput, calls=%fused_computation.28.clone.1 | convolution fusion | flops 104795392 | bytes 7487492 | tf_op jit(solution)/shard_map/while/body/eval_jaxpr/bthqk,btkhe->btqhe/dot_general | solution.py:31
  122.5 1.9 fusion.303
  125.4 7.4 %fusion.305 = bf16[1,4,256,6,64]{2,4,3,1,0:T(8,128)(2,1)} fusion(bf16[1,4,256,6,64]{2,4,3,1,0:T(8,128)(2,1)} %get-tuple-element.382, s32[]{:T(128)S(6)} %select_n.25, f32[4,6,128]{2,1,0:T(8,128)S(1)} %fusion.304, bf16[1,4,256,6,64]{2,4,3,1,0:T(8,128)(2,1)} %get-tuple-element.394, f32[4,6,128,256]{3,2,1,0:T(8,128)S(1)} %fusion.303), kind=kOutput, calls=%fused_computation.28.clone.1 | convolution fusion | flops 104795392 | bytes 7487492 | tf_op jit(solution)/shard_map/while/body/eval_jaxpr/bthqk,btkhe->btqhe/dot_general | solution.py:31
  133.0 2.6 %convert_reduce_fusion.1 = (f32[4,256]{1,0:T(4,128)S(1)}, bf16[4,256,384]{2,1,0:T(8,128)(2,1)S(1)}) fusion(f32[4,256,384]{2,1,0:T(8,128)} %bitcast.313, bf16[4,6,64,384]{3,2,1,0:T(8,128)(2,1)} %param.13, bf16[1,4,256,6,64]{2,4,3,1,0:T(8,128)(2,1)} %get-tuple-element.230), kind=kOutput, calls=%fused_computation.89 | convolution fusion | flops 303561728 | bytes 3444736 | tf_op jit(solution)/shard_map/btshe,hed->btsd/dot_general | solution.py:44
  136.1 5.2 %fusion.161 = bf16[1,4,256,384]{3,2,1,0:T(8,128)(2,1)S(1)} fusion(bf16[4,256,384]{2,1,0:T(8,128)(2,1)S(1)} %get-tuple-element.280, bf16[4,1536,384]{2,1,0:T(8,128)(2,1)} %param.15, bf16[4,384,1536]{2,1,0:T(8,128)(2,1)} %param.14, f32[384]{0:T(512)S(1)} %get-tuple-element.234, f32[384]{0:T(512)S(1)} %get-tuple-element.235, ...), kind=kOutput, calls=%fused_computation.192 | convolution fusion | flops 2433613824 | bytes 4730880 | tf_op jit(solution)/shard_map/btsf,fd->btsd/dot_general | solution.py:49
  141.9 14.3 %all_to_all.13 = bf16[1,4,256,384]{3,1,0,2:T(4,128)(2,1)S(1)} all-to-all(bf16[1,4,256,384]{3,1,0,2:T(4,128)(2,1)S(1)} %copy.79), channel_id=1, replica_groups=mesh['data'=4,'sp'=4] {'sp'}, dimensions={2} | all-to-all | bytes 1572864 | tf_op jit(solution)/shard_map/all_to_all | solution.py:58
  161.4 3.5 %fusion.131 = f32[64,6,16,16]{2,3,1,0:T(8,128)S(1)} fusion(bf16[16,64,6,64]{3,1,2,0:T(8,128)(2,1)S(1)} %convolution_convert_fusion.1, bf16[16,64,6,64]{3,1,2,0:T(8,128)(2,1)S(1)} %convolution_convert_fusion.2), kind=kOutput, calls=%fused_computation.158 | convolution fusion | flops 12582912 | bytes 1966080 | tf_op jit(solution)/shard_map/while/body/eval_jaxpr/bqshe,bkshe->bshqk/dot_general | solution.py:29
  164.9 12.4 %fusion.268 = (f32[64,6,16]{2,1,0:T(8,128)S(1)}, f32[64,6,16,16]{2,3,1,0:T(8,128)S(1)}) fusion(f32[64,6,16,16]{2,3,1,0:T(8,128)S(1)} %fusion.131), kind=kOutput, calls=%fused_computation.312 | output fusion | flops 393231 | bytes 811008 | tf_op jit(solution)/shard_map/while/body/eval_jaxpr/sub | solution.py:30
  177.3 1.8 fusion.147
  179.2 1.9 fusion.125
  181.8 6.1 %fusion.160 = bf16[1,16,64,384]{3,2,1,0:T(8,128)(2,1)} fusion(bf16[16,64,384]{2,1,0:T(8,128)(2,1)S(1)} %fusion.125, bf16[4,1536,384]{2,1,0:T(8,128)(2,1)} %param.15, bf16[4,384,1536]{2,1,0:T(8,128)(2,1)} %param.14, f32[384]{0:T(512)S(1)} %get-tuple-element.246, f32[384]{0:T(512)S(1)} %get-tuple-element.231, f32[16,64]{1,0:T(8,128)S(1)} %add_rsqrt_fusion, ...), kind=kOutput, calls=%fused_computation.191 | convolution fusion | flops 2433613824 | bytes 4739072 | tf_op jit(solution)/shard_map/btsf,fd->btsd/dot_general | solution.py:49
  (70 shorter events, 28.6 us)
Async XLA Ops:
  0.0 3.7 %copy-start.4 = (f32[4,4,384]{2,1,0:T(4,128)S(1)}, f32[4,4,384]{2,1,0:T(4,128)}, u32[]{:S(2)}) copy-start(f32[4,4,384]{2,1,0:T(4,128)} %param.11) | copy-start | bytes 73732
  0.0 3.8 %copy-start.1 = (bf16[1,4,256,384]{3,2,1,0:T(8,128)(2,1)S(1)}, bf16[1,4,256,384]{3,2,1,0:T(8,128)(2,1)}, u32[]{:S(2)}) copy-start(bf16[1,4,256,384]{3,2,1,0:T(8,128)(2,1)} %param.10) | copy-start | bytes 2359300
  57.2 1.2 copy-start.3
  88.3 15.0 %all-to-all-start.1 = ((bf16[1,16,64,384]{3,2,0,1:T(8,128)(2,1)}), bf16[1,16,64,384]{3,2,0,1:T(8,128)(2,1)S(1)}, u32[]{:S(2)}, u32[]{:S(2)}) async-start(bf16[1,16,64,384]{3,2,0,1:T(8,128)(2,1)} %fusion.162), calls=%async_computation.1 | async-start | bytes 1572864 | tf_op jit(solution)/shard_map/all_to_all | solution.py:62
  104.2 1.2 copy-start
  157.1 1.2 copy-start.2
where the time goes:
time: 192 us; the launch traced here: 188 us
  matrix products  94.5 us (49%)
  other arithmetic  36.2 us (19%)
  blocking collectives  30.5 us (16%)
  waiting for transfers between devices  11.4 us (6%)
  local copies, waits for them, and re-layouts  10.7 us (6%)
  starting transfers between devices  3.67 us (2%)
    dot_general x6, matrix products, attend_block(): jnp.einsum(mix_form, attn_probs, value_rows, preferred_element_type=jnp.f...  33.2 us
    all_to_all x2, blocking collectives, local_stack(): tokens = lax.all_to_all(tokens, 'sp', 2, 1, tiled=True)  30.5 us
    sub x6, other arithmetic, attend_block(): attn_probs = jax.nn.softmax(logits, axis=-1).astype(jnp.bfloat16)  29.4 us
    dot_general x4, matrix products, transformer_block(): jnp.einsum('btsf,fd->btsd', hidden, down_weight, preferred_element_type=j...  22.7 us
    dot_general x12, matrix products, project_heads(): jnp.einsum('btsd,dhe->btshe', normed, head_weight, preferred_element_type...  15.4 us
    dot_general x6, matrix products, attend_block(): jnp.einsum(score_form, q_part, key_rows, preferred_element_type=jnp.float32)  14.6 us
    all_to_all x1, waiting for transfers between devices, local_stack(): tokens = lax.all_to_all(tokens, 'sp', 1, 2, tiled=True)  11.4 us
    dot_general x4, matrix products, transformer_block(): jnp.einsum('btshe,hed->btsd', mixed_heads, out_weight, preferred_element_...  8.59 us
  transfers between devices with their start and end apart: 1, of which 1 were waited for; matrix products, arithmetic and copies ran while one was open for 0% of the time, Pallas kernels for 0%

commit v1 on v0

v1 whole, which is shorter than its diff:
```python
import jax
import jax.numpy as jnp
from jax import lax
from jax.experimental import pallas as pl
from jax.experimental.pallas import tpu as pltpu
from jax.sharding import PartitionSpec as P

F32, BF16 = jnp.float32, jnp.bfloat16
EPS = 1e-6
WIDTH, HEAD_DIM, HIDDEN = 384, 64, 1536
NT = (((1,), (1,)), ((), ()))
NN = (((1,), (0,)), ((), ()))
TN = (((0,), (0,)), ((), ()))
SCORE_SCALE = 0.125 * 1.4426950408889634
MESH = pl.DeviceIdType.MESH


def dot(a, b, dims):
    return lax.dot_general(a, b, dims, preferred_element_type=F32)


def layer_norm(x, gain, shift):
    centered = x - jnp.sum(x, -1, keepdims=True) * (1.0 / WIDTH)
    variance = jnp.sum(centered * centered, -1, keepdims=True) * (1.0 / WIDTH)
    return (centered * lax.rsqrt(variance + EPS) * gain + shift).astype(BF16)


def gelu(x):
    c = 0.7978845608028654
    half = 0.5 * x
    return (half + half * jnp.tanh(x * (c + (c * 0.044715) * (x * x)))).astype(BF16)


def softmax_keys(scores, mask=None):
    if mask is not None:
        scores = jnp.where(mask, scores, -jnp.inf)
    peak = jnp.max(scores, 0, keepdims=True)
    e = jnp.exp2((scores - peak) * SCORE_SCALE)
    return (e * (1.0 / jnp.sum(e, 0, keepdims=True))).astype(BF16)


def swap_halves(x, a, b):
    return x.reshape(a, b, 8, WIDTH).transpose(1, 0, 2, 3).reshape(256, WIDTH)


def block(u, l, norms, wq, wo, wu, wd, hid, temporal):
    x = u.astype(F32)
    if temporal:
        x = swap_halves(x, 16, 2)
    a = layer_norm(x, norms[l, 0:1, :], norms[l, 1:2, :])
    qT = dot(wq[l, 0:384, :], a, NT).astype(BF16)
    k = dot(a, wq[l, 384:768, :], NT).astype(BF16)
    vT = dot(wq[l, 768:1152, :], a, NT).astype(BF16)
    outs = []
    if not temporal:
        zero = jnp.zeros((64, 256), BF16)
        for p in range(3):
            kp = k[:, 128 * p:128 * p + 128]
            for j in range(2):
                h = 64 * (2 * p + j)
                qh = qT[h:h + 64, :]
                rhs = jnp.concatenate([qh, zero] if j == 0 else [zero, qh], 0)
                pT = softmax_keys(dot(kp, rhs, NN))
                outs.append(dot(vT[h:h + 64, :], pT, NN).astype(BF16))
    else:
        zero = jnp.zeros((64, 128), BF16)
        row = lax.broadcasted_iota(jnp.int32, (128, 256), 0)
        col = lax.broadcasted_iota(jnp.int32, (128, 256), 1)
        mask = (row & 7) == (col & 7)
        for p in range(3):
            h = 128 * p
            even, odd = [], []
            for i in range(2):
                t = 128 * i
                q0 = jnp.concatenate([qT[h:h + 64, t:t + 128], zero], 1)
                q1 = jnp.concatenate([zero, qT[h + 64:h + 128, t:t + 128]], 1)
                scores = dot(k[t:t + 128, h:h + 128], jnp.concatenate([q0, q1], 0), NN)
                pT = softmax_keys(scores, mask)
                o = dot(vT[h:h + 128, t:t + 128], pT, NN).astype(BF16)
                even.append(o[0:64, 0:128])
                odd.append(o[64:128, 128:256])
            outs += [jnp.concatenate(even, 1), jnp.concatenate(odd, 1)]
    oT = jnp.concatenate(outs, 0)
    res = (x + dot(oT, wo[l], TN)).astype(BF16).astype(F32)
    a2 = layer_norm(res, norms[l, 2:3, :], norms[l, 3:4, :])
    for c in range(0, HIDDEN, 512):
        hid[:, c:c + 512] = gelu(dot(a2, wu[l, :, c:c + 512], NN))
    z = res + dot(hid[...], wd[l], NN)
    if temporal:
        z = swap_halves(z, 2, 16)
    return z.astype(BF16)


def kernel(x_hbm, norms, wq_hbm, wo_hbm, wu_hbm, wd_hbm, y_hbm,
           xb, wq, wo, wu, wd, hid, frames0, frames1, frames2, cols0, cols1, cols2,
           load_sem, send_sem, recv_sem):
    me = lax.axis_index('sp')
    loads = []
    for l in range(4):
        pairs = ((wq_hbm, wq), (wo_hbm, wo), (wu_hbm, wu), (wd_hbm, wd))
        loads.append([pltpu.make_async_copy(s.at[l], d.at[l], load_sem.at[l, i]) for i, (s, d) in enumerate(pairs)])
    x_load = pltpu.make_async_copy(x_hbm, xb, load_sem.at[4, 0])
    x_load.start()
    for group in loads:
        for c in group:
            c.start()
    barrier = pltpu.get_barrier_semaphore()
    for d in range(1, 4):
        pl.semaphore_signal(barrier, inc=1, device_id={'sp': (me + d) % 4}, device_id_type=MESH)
    pl.semaphore_wait(barrier, 3)
    x_load.wait()

    def to_columns(e, src, dst, f, d):
        peer = (me + d) % 4
        rows = pl.ds(pl.multiple_of(64 * peer, 64), 64)
        return pltpu.make_async_remote_copy(
            src_ref=src.at[f, rows, :], dst_ref=dst.at[4 * me + f],
            send_sem=send_sem.at[e, f, d - 1], recv_sem=recv_sem.at[e, f, d - 1],
            device_id={'sp': peer}, device_id_type=MESH)

    def to_frames(e, src, dst, g, d):
        peer = (me + d) % 4
        return pltpu.make_async_remote_copy(
            src_ref=src.at[pl.ds(4 * peer, 4), pl.ds(pl.multiple_of(16 * g, 16), 16), :],
            dst_ref=dst.at[:, pl.ds(pl.multiple_of(64 * me + 16 * g, 16), 16), :],
            send_sem=send_sem.at[e, g, d - 1], recv_sem=recv_sem.at[e, g, d - 1],
            device_id={'sp': peer}, device_id_type=MESH)

    def spatial(l, e, src, out, dst):
        def body(f, _):
            z = block(src[f], l, norms, wq, wo, wu, wd, hid, False)
            out[f] = z
            for d in range(1, 4):
                to_columns(e, out, dst, f, d).start()
            dst[4 * me + f] = out[f, pl.ds(pl.multiple_of(64 * me, 64), 64), :]
            return 0
        lax.fori_loop(0, 4, body, 0)

    def wait_all(e, make, src, dst):
        for f in range(4):
            for d in range(1, 4):
                c = make(e, src, dst, f, d)
                c.wait_recv()
                c.wait_send()

    def temporal(l, e, src, out, dst):
        def body(g, _):
            cols = pl.ds(pl.multiple_of(16 * g, 16), 16)
            z = block(src[:, cols, :].reshape(256, WIDTH), l, norms, wq, wo, wu, wd, hid, True)
            out[:, cols, :] = z.reshape(16, 16, WIDTH)
            if dst is not None:
                for d in range(1, 4):
                    to_frames(e, out, dst, g, d).start()
                mine = pl.ds(pl.multiple_of(64 * me + 16 * g, 16), 16)
                dst[:, mine, :] = out[pl.ds(4 * me, 4), cols, :]
            return 0
        lax.fori_loop(0, 4, body, 0)

    def wait_weights(l):
        for c in loads[l]:
            c.wait()

    wait_weights(0)
    spatial(0, 0, xb, frames0, cols0)
    wait_weights(1)
    wait_all(0, to_columns, frames0, cols0)
    temporal(1, 1, cols0, cols1, frames1)
    wait_weights(2)
    wait_all(1, to_frames, cols1, frames1)
    spatial(2, 2, frames1, frames2, cols2)
    wait_weights(3)
    wait_all(2, to_columns, frames2, cols2)
    temporal(3, 3, cols2, cols0, None)
    y_store = pltpu.make_async_copy(cols0, y_hbm, load_sem.at[4, 1])
    y_store.start()
    y_store.wait()


def solution(mesh):
    anyspace = pl.BlockSpec(memory_space=pl.ANY)

    def local_stack(latents, norms, w_qkv, w_out, w_up, w_down):
        frames = (4, 256, WIDTH)
        cols = (16, 64, WIDTH)
        out = pl.pallas_call(
            kernel,
            out_shape=jax.ShapeDtypeStruct(cols, BF16),
            in_specs=[anyspace, pl.BlockSpec(memory_space=pltpu.VMEM)] + [anyspace] * 4,
            out_specs=anyspace,
            scratch_shapes=[
                pltpu.VMEM(frames, BF16),
                pltpu.VMEM((4, 1152, WIDTH), BF16), pltpu.VMEM((4, WIDTH, WIDTH), BF16),
                pltpu.VMEM((4, WIDTH, HIDDEN), BF16), pltpu.VMEM((4, HIDDEN, WIDTH), BF16),
                pltpu.VMEM((256, HIDDEN), BF16),
                pltpu.VMEM(frames, BF16), pltpu.VMEM(frames, BF16), pltpu.VMEM(frames, BF16),
                pltpu.VMEM(cols, BF16), pltpu.VMEM(cols, BF16), pltpu.VMEM(cols, BF16),
                pltpu.SemaphoreType.DMA((5, 4)),
                pltpu.SemaphoreType.DMA((3, 4, 3)),
                pltpu.SemaphoreType.DMA((3, 4, 3)),
            ],
            compiler_params=pltpu.CompilerParams(collective_id=0, has_side_effects=True, vmem_limit_bytes=56 * 2**20),
        )(latents[0], norms,
          w_qkv.transpose(0, 2, 3, 4, 1).reshape(4, 3 * WIDTH, WIDTH),
          w_out.reshape(4, WIDTH, WIDTH), w_up, w_down)
        return out[None]

    whole = P()
    return jax.shard_map(local_stack, mesh=mesh,
                         in_specs=(P('data', 'sp', None, None), whole, whole, whole, whole, whole),
                         out_specs=P('data', None, 'sp', None), check_vma=False)
```

time: 192 us -> 74.8 us (0.39); the launches traced: 188 us -> 74.6 us
  matrix products: 94.5 us -> 0 us
  Pallas kernels: 0 us -> 72.5 us
  other arithmetic: 36.2 us -> 0 us
  blocking collectives: 30.5 us -> 0 us
  waiting for transfers between devices: 11.4 us -> 0 us
  local copies, waits for them, and re-layouts: 10.7 us -> 2.09 us
  starting transfers between devices: 3.67 us -> 0 us
    dot_general x32 -> x0, matrix products: 94.5 us -> none  [the longest x6 33.2 us: attend_block(): jnp.einsum(mix_form, attn_probs, value_rows, preferred_element_type=jnp.f...]
    pallas_call x0 -> x1, Pallas kernels: none -> 72.5 us  [local_stack(): pl.pallas_call(kernel, out_shape=jax.ShapeDtypeStruct(cols, BF16), in_spe...]
    all_to_all x2 -> x0, blocking collectives: 30.5 us -> none  [local_stack(): tokens = lax.all_to_all(tokens, 'sp', 2, 1, tiled=True)]
    sub x6 -> x0, other arithmetic: 29.4 us -> none  [attend_block(): attn_probs = jax.nn.softmax(logits, axis=-1).astype(jnp.bfloat16)]
    all_to_all x1 -> x0, waiting for transfers between devices: 11.4 us -> none  [local_stack(): tokens = lax.all_to_all(tokens, 'sp', 1, 2, tiled=True)]
    reduce_sum x14 -> x0, other arithmetic: 5.05 us -> none  [the longest x8 3.76 us: layer_norm(): variance = jnp.mean(jnp.square(centered), axis=-1, keepdims=True)]
    squeeze x1 -> x0, local copies, waits for them, and re-layouts: 3.73 us -> none  [local_stack(): w_qkv[layer_idx]]
    all_to_all x1 -> x0, starting transfers between devices: 3.67 us -> none  [local_stack(): tokens = lax.all_to_all(tokens, 'sp', 1, 2, tiled=True)]
  transfers between devices with their start and end apart: 1 -> 0, of which waited for: 1 -> 0; matrix products, arithmetic and copies ran while one was open for 0% -> 0% of each run, Pallas kernels for 0% -> 0%
where the time goes in v1:
time: 74.8 us; the launch traced here: 74.6 us
  Pallas kernels  72.5 us (97%)
  local copies, waits for them, and re-layouts  2.09 us (3%)
    pallas_call x1, Pallas kernels, local_stack(): pl.pallas_call(kernel, out_shape=jax.ShapeDtypeStruct(cols, BF16), in_spe...  72.5 us
    unnamed x1, local copies, waits for them, and re-layouts  2.09 us

profile of v1, /device:TPU:0, one launch (start us, length us, event | category | flops | bytes accessed | tf_op | source)
XLA Modules:
  0.0 74.6 jit_solution(9629669898575835573)
XLA Ops:
  0.0 72.5 %shard_map.64 = bf16[16,64,384]{2,1,0:T(8,128)(2,1)} custom-call(bf16[4,256,384]{2,1,0:T(8,128)(2,1)} %bitcast.9, f32[4,4,384]{2,1,0:T(4,128)} %norms.1, bf16[4,1152,384]{2,1,0:T(8,128)(2,1)} %bitcast.6, bf16[4,384,384]{2,1,0:T(8,128)(2,1)} %bitcast.8, bf16[4,384,1536]{2,1,0:T(8,128)(2,1)} %wu_hbm.1, bf16[4,1536,384]{2,1,0:T(8,128)(2,1)} %wd_hbm.1), custom_call_target="tpu_custom_call" | custom-call | tf_op jit(solution)/shard_map/pallas_call | solution.py:185
  72.5 2.1 %copy.8 = bf16[1,16,64,384]{3,2,1,0:T(8,128)(2,1)} copy(bf16[1,16,64,384]{3,2,1,0:T(8,128)(2,1)} %bitcast.7) | data formatting | bytes 1572864

commit v2 on v1

--- a/solution.py
+++ b/solution.py
@@ -31,19 +31,11 @@
     return (half + half * jnp.tanh(x * (c + (c * 0.044715) * (x * x)))).astype(BF16)
 
 
-def softmax_keys(scores, mask=None):
-    if mask is not None:
-        scores = jnp.where(mask, scores, -jnp.inf)
-    peak = jnp.max(scores, 0, keepdims=True)
-    e = jnp.exp2((scores - peak) * SCORE_SCALE)
-    return (e * (1.0 / jnp.sum(e, 0, keepdims=True))).astype(BF16)
-
-
 def swap_halves(x, a, b):
     return x.reshape(a, b, 8, WIDTH).transpose(1, 0, 2, 3).reshape(256, WIDTH)
 
 
-def block(u, l, norms, wq, wo, wu, wd, hid, temporal):
+def block(u, l, norms, wq, wo, wu, wd, hid, scratch, temporal):
     x = u.astype(F32)
     if temporal:
         x = swap_halves(x, 16, 2)
@@ -51,36 +43,42 @@
     qT = dot(wq[l, 0:384, :], a, NT).astype(BF16)
     k = dot(a, wq[l, 384:768, :], NT).astype(BF16)
     vT = dot(wq[l, 768:1152, :], a, NT).astype(BF16)
-    outs = []
+    scores, expd, probs, mixed = scratch
     if not temporal:
         zero = jnp.zeros((64, 256), BF16)
-        for p in range(3):
-            kp = k[:, 128 * p:128 * p + 128]
-            for j in range(2):
-                h = 64 * (2 * p + j)
-                qh = qT[h:h + 64, :]
-                rhs = jnp.concatenate([qh, zero] if j == 0 else [zero, qh], 0)
-                pT = softmax_keys(dot(kp, rhs, NN))
-                outs.append(dot(vT[h:h + 64, :], pT, NN).astype(BF16))
+        for h in range(6):
+            qh = qT[64 * h:64 * h + 64, :]
+            rhs = jnp.concatenate([zero, qh] if h % 2 else [qh, zero], 0)
+            p = h // 2 * 128
+            scores[h] = dot(k[:, p:p + 128], rhs, NN)
     else:
         zero = jnp.zeros((64, 128), BF16)
         row = lax.broadcasted_iota(jnp.int32, (128, 256), 0)
         col = lax.broadcasted_iota(jnp.int32, (128, 256), 1)
-        mask = (row & 7) == (col & 7)
-        for p in range(3):
-            h = 128 * p
-            even, odd = [], []
-            for i in range(2):
-                t = 128 * i
-                q0 = jnp.concatenate([qT[h:h + 64, t:t + 128], zero], 1)
-                q1 = jnp.concatenate([zero, qT[h + 64:h + 128, t:t + 128]], 1)
-                scores = dot(k[t:t + 128, h:h + 128], jnp.concatenate([q0, q1], 0), NN)
-                pT = softmax_keys(scores, mask)
-                o = dot(vT[h:h + 128, t:t + 128], pT, NN).astype(BF16)
-                even.append(o[0:64, 0:128])
-                odd.append(o[64:128, 128:256])
-            outs += [jnp.concatenate(even, 1), jnp.concatenate(odd, 1)]
-    oT = jnp.concatenate(outs, 0)
+        same_patch = (row & 7) == (col & 7)
+        for h in range(6):
+            p, t = h // 2 * 128, h % 2 * 128
+            q0 = jnp.concatenate([qT[p:p + 64, t:t + 128], zero], 1)
+            q1 = jnp.concatenate([zero, qT[p + 64:p + 128, t:t + 128]], 1)
+            s = dot(k[t:t + 128, p:p + 128], jnp.concatenate([q0, q1], 0), NN)
+            scores[h, 0:128] = jnp.where(same_patch, s, -jnp.inf)
+    keys = 128 if temporal else 256
+    for h in range(6):
+        peak = jnp.max(scores[h, 0:keys], 0, keepdims=True)
+        e = jnp.exp2((scores[h, 0:keys] - peak) * SCORE_SCALE)
+        expd[h, 0:keys] = e
+        inverse = 1.0 / jnp.sum(e, 0, keepdims=True)
+        probs[h, 0:keys] = (expd[h, 0:keys] * inverse).astype(BF16)
+    for h in range(6):
+        if not temporal:
+            r = 64 * h
+            mixed[r:r + 64, :] = dot(vT[r:r + 64, :], probs[h], NN).astype(BF16)
+        else:
+            p, t = h // 2 * 128, h % 2 * 128
+            o = dot(vT[p:p + 128, t:t + 128], probs[h, 0:128], NN).astype(BF16)
+            mixed[p:p + 64, t:t + 128] = o[0:64, 0:128]
+            mixed[p + 64:p + 128, t:t + 128] = o[64:128, 128:256]
+    oT = mixed[...]
     res = (x + dot(oT, wo[l], TN)).astype(BF16).astype(F32)
     a2 = layer_norm(res, norms[l, 2:3, :], norms[l, 3:4, :])
     for c in range(0, HIDDEN, 512):
@@ -93,7 +91,7 @@
 
 def kernel(x_hbm, norms, wq_hbm, wo_hbm, wu_hbm, wd_hbm, y_hbm,
            xb, wq, wo, wu, wd, hid, frames0, frames1, frames2, cols0, cols1, cols2,
-           load_sem, send_sem, recv_sem):
+           load_sem, send_sem, recv_sem, *scratch):
     me = lax.axis_index('sp')
     loads = []
     for l in range(4):
@@ -101,9 +99,8 @@
         loads.append([pltpu.make_async_copy(s.at[l], d.at[l], load_sem.at[l, i]) for i, (s, d) in enumerate(pairs)])
     x_load = pltpu.make_async_copy(x_hbm, xb, load_sem.at[4, 0])
     x_load.start()
-    for group in loads:
-        for c in group:
-            c.start()
+    for c in loads[0]:
+        c.start()
     barrier = pltpu.get_barrier_semaphore()
     for d in range(1, 4):
         pl.semaphore_signal(barrier, inc=1, device_id={'sp': (me + d) % 4}, device_id_type=MESH)
@@ -128,7 +125,7 @@
 
     def spatial(l, e, src, out, dst):
         def body(f, _):
-            z = block(src[f], l, norms, wq, wo, wu, wd, hid, False)
+            z = block(src[f], l, norms, wq, wo, wu, wd, hid, scratch, False)
             out[f] = z
             for d in range(1, 4):
                 to_columns(e, out, dst, f, d).start()
@@ -146,7 +143,7 @@
     def temporal(l, e, src, out, dst):
         def body(g, _):
             cols = pl.ds(pl.multiple_of(16 * g, 16), 16)
-            z = block(src[:, cols, :].reshape(256, WIDTH), l, norms, wq, wo, wu, wd, hid, True)
+            z = block(src[:, cols, :].reshape(256, WIDTH), l, norms, wq, wo, wu, wd, hid, scratch, True)
             out[:, cols, :] = z.reshape(16, 16, WIDTH)
             if dst is not None:
                 for d in range(1, 4):
@@ -161,6 +158,9 @@
             c.wait()
 
     wait_weights(0)
+    for group in loads[1:]:
+        for c in group:
+            c.start()
     spatial(0, 0, xb, frames0, cols0)
     wait_weights(1)
     wait_all(0, to_columns, frames0, cols0)
@@ -197,6 +197,8 @@
                 pltpu.SemaphoreType.DMA((5, 4)),
                 pltpu.SemaphoreType.DMA((3, 4, 3)),
                 pltpu.SemaphoreType.DMA((3, 4, 3)),
+                pltpu.VMEM((6, 256, 256), F32), pltpu.VMEM((6, 256, 256), F32),
+                pltpu.VMEM((6, 256, 256), BF16), pltpu.VMEM((WIDTH, 256), BF16),
             ],
             compiler_params=pltpu.CompilerParams(collective_id=0, has_side_effects=True, vmem_limit_bytes=56 * 2**20),
         )(latents[0], norms,

time: 74.8 us -> 62.4 us (0.83)
  Pallas kernels: 72.5 us -> 60.1 us
    pallas_call x1, Pallas kernels: 72.5 us -> 60.1 us  [local_stack(): pl.pallas_call(kernel, out_shape=jax.ShapeDtypeStruct(cols, BF16), in_spe...]
where the time goes in v2:
time: 62.4 us; the launch traced here: 62.2 us
  Pallas kernels  60.1 us (96%)
  local copies, waits for them, and re-layouts  2.09 us (3%)
    pallas_call x1, Pallas kernels, local_stack(): pl.pallas_call(kernel, out_shape=jax.ShapeDtypeStruct(cols, BF16), in_spe...  60.1 us
    unnamed x1, local copies, waits for them, and re-layouts  2.09 us

profile of v2, /device:TPU:0, one launch (start us, length us, event | category | flops | bytes accessed | tf_op | source)
XLA Modules:
  0.0 62.2 jit_solution(4352012291472615930)
XLA Ops:
  0.0 60.1 %shard_map.64 = bf16[16,64,384]{2,1,0:T(8,128)(2,1)} custom-call(bf16[4,256,384]{2,1,0:T(8,128)(2,1)} %bitcast.9, f32[4,4,384]{2,1,0:T(4,128)} %norms.1, bf16[4,1152,384]{2,1,0:T(8,128)(2,1)} %bitcast.6, bf16[4,384,384]{2,1,0:T(8,128)(2,1)} %bitcast.8, bf16[4,384,1536]{2,1,0:T(8,128)(2,1)} %wu_hbm.1, bf16[4,1536,384]{2,1,0:T(8,128)(2,1)} %wd_hbm.1), custom_call_target="tpu_custom_call" | custom-call | tf_op jit(solution)/shard_map/pallas_call | solution.py:185
  60.1 2.1 %copy.8 = bf16[1,16,64,384]{3,2,1,0:T(8,128)(2,1)} copy(bf16[1,16,64,384]{3,2,1,0:T(8,128)(2,1)} %bitcast.7) | data formatting | bytes 1572864

commit v3 on v2

v3 whole, which is shorter than its diff:
```python
import jax
import jax.numpy as jnp
from jax import lax
from jax.experimental import pallas as pl
from jax.experimental.pallas import tpu as pltpu
from jax.sharding import PartitionSpec as P

F32, BF16 = jnp.float32, jnp.bfloat16
EPS = 1e-6
WIDTH, HIDDEN = 384, 1536
NT = (((1,), (1,)), ((), ()))
NN = (((1,), (0,)), ((), ()))
TN = (((0,), (0,)), ((), ()))
SCORE_SCALE = 0.125 * 1.4426950408889634
MESH = pl.DeviceIdType.MESH


def dot(a, b, dims):
    return lax.dot_general(a, b, dims, preferred_element_type=F32)


def layer_norm(x, gain, shift):
    centered = x - jnp.sum(x, -1, keepdims=True) * (1.0 / WIDTH)
    variance = jnp.sum(centered * centered, -1, keepdims=True) * (1.0 / WIDTH)
    return (centered * lax.rsqrt(variance + EPS) * gain + shift).astype(BF16)


def gelu(x):
    c = 0.7978845608028654
    half = 0.5 * x
    return (half + half * jnp.tanh(x * (c + (c * 0.044715) * (x * x)))).astype(BF16)


def swap_halves(x, a, b):
    return x.reshape(a, b, 8, WIDTH).transpose(1, 0, 2, 3).reshape(256, WIDTH)


def head_scores(qT, k, scores, temporal):
    if not temporal:
        zero = jnp.zeros((64, 256), BF16)
        for h in range(6):
            qh = qT[64 * h:64 * h + 64, :]
            rhs = jnp.concatenate([zero, qh] if h % 2 else [qh, zero], 0)
            p = h // 2 * 128
            scores[h] = dot(k[:, p:p + 128], rhs, NN)
    else:
        zero = jnp.zeros((64, 128), BF16)
        row = lax.broadcasted_iota(jnp.int32, (128, 256), 0)
        col = lax.broadcasted_iota(jnp.int32, (128, 256), 1)
        same_patch = (row & 7) == (col & 7)
        for h in range(6):
            p, t = h // 2 * 128, h % 2 * 128
            q0 = jnp.concatenate([qT[p:p + 64, t:t + 128], zero], 1)
            q1 = jnp.concatenate([zero, qT[p + 64:p + 128, t:t + 128]], 1)
            s = dot(k[t:t + 128, p:p + 128], jnp.concatenate([q0, q1], 0), NN)
            scores[h, 0:128] = jnp.where(same_patch, s, -jnp.inf)


def head_probs(scores, expd, probs, temporal):
    keys = 128 if temporal else 256
    for h in range(6):
        peak = jnp.max(scores[h, 0:keys], 0, keepdims=True)
        e = jnp.exp2((scores[h, 0:keys] - peak) * SCORE_SCALE)
        expd[h, 0:keys] = e
        inverse = 1.0 / jnp.sum(e, 0, keepdims=True)
        probs[h, 0:keys] = (expd[h, 0:keys] * inverse).astype(BF16)


def head_mix(vT, probs, mixed, temporal):
    for h in range(6):
        if not temporal:
            r = 64 * h
            mixed[r:r + 64, :] = dot(vT[r:r + 64, :], probs[h], NN).astype(BF16)
        else:
            p, t = h // 2 * 128, h % 2 * 128
            o = dot(vT[p:p + 128, t:t + 128], probs[h, 0:128], NN).astype(BF16)
            mixed[p:p + 64, t:t + 128] = o[0:64, 0:128]
            mixed[p + 64:p + 128, t:t + 128] = o[64:128, 128:256]


def attend(xs, l, norms, wq, wo, scratch, temporal):
    kept = []
    for j, x in enumerate(xs):
        a = layer_norm(x, norms[l, 0:1, :], norms[l, 1:2, :])
        qT = dot(wq[l, 0:384, :], a, NT).astype(BF16)
        k = dot(a, wq[l, 384:768, :], NT).astype(BF16)
        kept.append(dot(wq[l, 768:1152, :], a, NT).astype(BF16))
        head_scores(qT, k, scratch[0].at[j], temporal)
    for j in range(len(xs)):
        head_probs(scratch[0].at[j], scratch[1].at[j], scratch[2].at[j], temporal)
    for j in range(len(xs)):
        head_mix(kept[j], scratch[2].at[j], scratch[3].at[j], temporal)
    return [(x + dot(scratch[3][j], wo[l], TN)).astype(BF16) for j, x in enumerate(xs)]


def mlp(res, l, norms, wu, wd, hid):
    res = res.astype(F32)
    a = layer_norm(res, norms[l, 2:3, :], norms[l, 3:4, :])
    for c in range(0, HIDDEN, 512):
        hid[:, c:c + 512] = gelu(dot(a, wu[l, :, c:c + 512], NN))
    return res + dot(hid[...], wd[l], NN)


def kernel(x_hbm, norms, wq_hbm, wo_hbm, wu_hbm, wd_hbm, y_hbm,
           xb, wq, wo, wu, wd, hid, res, sent0, cols1, sent1, frames2, sent2, cols3, yb,
           load_sem, send_sem, recv_sem, *scratch):
    me = lax.axis_index('sp')
    pairs = ((wq_hbm, wq), (wo_hbm, wo), (wu_hbm, wu), (wd_hbm, wd))
    loads = [[pltpu.make_async_copy(s.at[l], d.at[l], load_sem.at[l, i]) for i, (s, d) in enumerate(pairs)]
             for l in range(4)]
    x_load = pltpu.make_async_copy(x_hbm, xb, load_sem.at[4, 0])
    x_load.start()
    for c in loads[0]:
        c.start()
    barrier = pltpu.get_barrier_semaphore()
    for d in range(1, 4):
        pl.semaphore_signal(barrier, inc=1, device_id={'sp': (me + d) % 4}, device_id_type=MESH)
    pl.semaphore_wait(barrier, 3)

    def to_columns(e, src, dst, g, d):
        peer = (me + d) % 4
        return pltpu.make_async_remote_copy(
            src_ref=src.at[g, peer], dst_ref=dst.at[g, pl.ds(4 * me, 4)],
            send_sem=send_sem.at[e, g, d - 1], recv_sem=recv_sem.at[e, g, d - 1],
            device_id={'sp': peer}, device_id_type=MESH)

    def to_frames(e, src, dst, g, d):
        peer = (me + d) % 4
        return pltpu.make_async_remote_copy(
            src_ref=src.at[g, pl.ds(4 * peer, 4)], dst_ref=dst.at[me, g],
            send_sem=send_sem.at[e, g, d - 1], recv_sem=recv_sem.at[e, g, d - 1],
            device_id={'sp': peer}, device_id_type=MESH)

    def spatial(l, e, read_frame, sent, dst):
        def attention_pair(i, _):
            rows = attend([read_frame(2 * i + j).astype(F32) for j in range(2)], l, norms, wq, wo, scratch, False)
            for j in range(2):
                res[2 * i + j] = rows[j].reshape(4, 4, 16, WIDTH)
            return 0

        def mlp_group(g, _):
            rows = jnp.stack([res[:, j, g] for j in range(4)])
            z = mlp(rows.reshape(256, WIDTH), l, norms, wu, wd, hid)
            sent[g] = z.astype(BF16).reshape(4, 4, 16, WIDTH)
            for d in (2, 1, 3):
                to_columns(e, sent, dst, g, d).start()
            dst[g, pl.ds(4 * me, 4)] = sent[g, me]
            return 0

        lax.fori_loop(0, 2, attention_pair, 0)
        lax.fori_loop(0, 4, mlp_group, 0)

    def temporal(l, e, src, write):
        def body(g, _):
            for d in (1, 2, 3):
                to_columns(e, sent0, src, g, d).wait_recv()
            x = swap_halves(src[g].reshape(256, WIDTH).astype(F32), 16, 2)
            rows = attend([x], l, norms, wq, wo, scratch, True)
            z = mlp(rows[0], l, norms, wu, wd, hid)
            write(g, swap_halves(z, 2, 16).astype(BF16).reshape(16, 16, WIDTH))
            return 0
        lax.fori_loop(0, 4, body, 0)

    def send_to_frames(g, z):
        sent1[g] = z
        for d in (2, 1, 3):
            to_frames(1, sent1, frames2, g, d).start()
        frames2[me, g] = sent1[g, pl.ds(4 * me, 4)]

    def y_store(g):
        return pltpu.make_async_copy(yb.at[g], y_hbm.at[:, pl.ds(pl.multiple_of(16 * g, 16), 16), :],
                                     load_sem.at[5, g])

    def write_y(g, z):
        yb[g] = z
        y_store(g).start()

    def wait_weights(l):
        for c in loads[l]:
            c.wait()

    x_load.wait()
    wait_weights(0)
    for group in loads[1:]:
        for c in group:
            c.start()
    spatial(0, 0, lambda f: xb[f], sent0, cols1)
    wait_weights(1)
    temporal(1, 0, cols1, send_to_frames)
    wait_weights(2)
    for g in range(4):
        for d in (1, 2, 3):
            to_frames(1, sent1, frames2, g, d).wait_recv()
    spatial(2, 2, lambda f: frames2[:, :, f].reshape(256, WIDTH), sent2, cols3)
    wait_weights(3)
    temporal(3, 2, cols3, write_y)
    for g in range(4):
        y_store(g).wait()
        for d in (1, 2, 3):
            to_columns(0, sent0, cols1, g, d).wait_send()
            to_frames(1, sent1, frames2, g, d).wait_send()
            to_columns(2, sent2, cols3, g, d).wait_send()


def solution(mesh):
    anyspace = pl.BlockSpec(memory_space=pl.ANY)

    def local_stack(latents, norms, w_qkv, w_out, w_up, w_down):
        tokens = (4, 4, 4, 16, WIDTH)
        groups = (4, 16, 16, WIDTH)
        out = pl.pallas_call(
            kernel,
            out_shape=jax.ShapeDtypeStruct((16, 64, WIDTH), BF16),
            in_specs=[anyspace, pl.BlockSpec(memory_space=pltpu.VMEM)] + [anyspace] * 4,
            out_specs=anyspace,
            scratch_shapes=[
                pltpu.VMEM((4, 256, WIDTH), BF16),
                pltpu.VMEM((4, 1152, WIDTH), BF16), pltpu.VMEM((4, WIDTH, WIDTH), BF16),
                pltpu.VMEM((4, WIDTH, HIDDEN), BF16), pltpu.VMEM((4, HIDDEN, WIDTH), BF16),
                pltpu.VMEM((256, HIDDEN), BF16),
                pltpu.VMEM(tokens, BF16),
                pltpu.VMEM(tokens, BF16), pltpu.VMEM(groups, BF16),
                pltpu.VMEM(groups, BF16), pltpu.VMEM(tokens, BF16),
                pltpu.VMEM(tokens, BF16), pltpu.VMEM(groups, BF16),
                pltpu.VMEM(groups, BF16),
                pltpu.SemaphoreType.DMA((6, 4)),
                pltpu.SemaphoreType.DMA((3, 4, 3)),
                pltpu.SemaphoreType.DMA((3, 4, 3)),
                pltpu.VMEM((2, 6, 256, 256), F32), pltpu.VMEM((2, 6, 256, 256), F32),
                pltpu.VMEM((2, 6, 256, 256), BF16), pltpu.VMEM((2, WIDTH, 256), BF16),
            ],
            compiler_params=pltpu.CompilerParams(collective_id=0, has_side_effects=True, vmem_limit_bytes=56 * 2**20),
        )(latents[0], norms,
          w_qkv.transpose(0, 2, 3, 4, 1).reshape(4, 3 * WIDTH, WIDTH),
          w_out.reshape(4, WIDTH, WIDTH), w_up, w_down)
        return out[None]

    whole = P()
    return jax.shard_map(local_stack, mesh=mesh,
                         in_specs=(P('data', 'sp', None, None), whole, whole, whole, whole, whole),
                         out_specs=P('data', None, 'sp', None), check_vma=False)
```

time: 62.4 us -> 53.4 us (0.86)
  Pallas kernels: 60.1 us -> 50.7 us
    pallas_call x1, Pallas kernels: 60.1 us -> 50.7 us  [local_stack(): pl.pallas_call(kernel, out_shape=jax.ShapeDtypeStruct((16, 64, WIDTH), BF...]
where the time goes in v3:
time: 53.4 us; the launch traced here: 52.8 us
  Pallas kernels  50.7 us (95%)
  local copies, waits for them, and re-layouts  2.09 us (4%)
    pallas_call x1, Pallas kernels, local_stack(): pl.pallas_call(kernel, out_shape=jax.ShapeDtypeStruct((16, 64, WIDTH), BF...  50.7 us
    unnamed x1, local copies, waits for them, and re-layouts  2.09 us

profile of v3, /device:TPU:0, one launch (start us, length us, event | category | flops | bytes accessed | tf_op | source)
XLA Modules:
  0.0 52.8 jit_solution(7218214383933899842)
XLA Ops:
  0.0 50.7 %shard_map.64 = bf16[16,64,384]{2,1,0:T(8,128)(2,1)} custom-call(bf16[4,256,384]{2,1,0:T(8,128)(2,1)} %bitcast.9, f32[4,4,384]{2,1,0:T(4,128)} %norms.1, bf16[4,1152,384]{2,1,0:T(8,128)(2,1)} %bitcast.6, bf16[4,384,384]{2,1,0:T(8,128)(2,1)} %bitcast.8, bf16[4,384,1536]{2,1,0:T(8,128)(2,1)} %wu_hbm.1, bf16[4,1536,384]{2,1,0:T(8,128)(2,1)} %wd_hbm.1), custom_call_target="tpu_custom_call" | custom-call | tf_op jit(solution)/shard_map/pallas_call | solution.py:211
  50.7 2.1 %copy.8 = bf16[1,16,64,384]{3,2,1,0:T(8,128)(2,1)} copy(bf16[1,16,64,384]{3,2,1,0:T(8,128)(2,1)} %bitcast.7) | data formatting | bytes 1572864

commit v4 on v3

--- a/solution.py
+++ b/solution.py
@@ -78,19 +78,33 @@
             mixed[p + 64:p + 128, t:t + 128] = o[64:128, 128:256]
 
 
+def head_scores_rows(q, k, scores):
+    low = lax.broadcasted_iota(jnp.int32, (256, 128), 1) < 64
+    for h in range(6):
+        p = h // 2 * 128
+        qp = q[:, p:p + 128]
+        zero = jnp.zeros_like(qp)
+        rhs = jnp.where(low, zero, qp) if h % 2 else jnp.where(low, qp, zero)
+        scores[h] = dot(k[:, p:p + 128], rhs, NT)
+
+
+def attend_end(xs, values, l, wo, scratch, temporal):
+    for j in range(len(xs)):
+        head_probs(scratch[0].at[j], scratch[1].at[j], scratch[2].at[j], temporal)
+    for j in range(len(xs)):
+        head_mix(values[j], scratch[2].at[j], scratch[3].at[j], temporal)
+    return [(x + dot(scratch[3][j], wo[l], TN)).astype(BF16) for j, x in enumerate(xs)]
+
+
 def attend(xs, l, norms, wq, wo, scratch, temporal):
-    kept = []
+    values = []
     for j, x in enumerate(xs):
         a = layer_norm(x, norms[l, 0:1, :], norms[l, 1:2, :])
         qT = dot(wq[l, 0:384, :], a, NT).astype(BF16)
         k = dot(a, wq[l, 384:768, :], NT).astype(BF16)
-        kept.append(dot(wq[l, 768:1152, :], a, NT).astype(BF16))
+        values.append(dot(wq[l, 768:1152, :], a, NT).astype(BF16))
         head_scores(qT, k, scratch[0].at[j], temporal)
-    for j in range(len(xs)):
-        head_probs(scratch[0].at[j], scratch[1].at[j], scratch[2].at[j], temporal)
-    for j in range(len(xs)):
-        head_mix(kept[j], scratch[2].at[j], scratch[3].at[j], temporal)
-    return [(x + dot(scratch[3][j], wo[l], TN)).astype(BF16) for j, x in enumerate(xs)]
+    return attend_end(xs, values, l, wo, scratch, temporal)
 
 
 def mlp(res, l, norms, wu, wd, hid):
@@ -102,7 +116,7 @@
 
 
 def kernel(x_hbm, norms, wq_hbm, wo_hbm, wu_hbm, wd_hbm, y_hbm,
-           xb, wq, wo, wu, wd, hid, res, sent0, cols1, sent1, frames2, sent2, cols3, yb,
+           xb, wq, wo, wu, wd, hid, res, sent0, cols1, sent1, frames2, sent2, cols3, yb, normed, queries, keys,
            load_sem, send_sem, recv_sem, *scratch):
     me = lax.axis_index('sp')
     pairs = ((wq_hbm, wq), (wo_hbm, wo), (wu_hbm, wu), (wd_hbm, wd))
@@ -110,7 +124,7 @@
              for l in range(4)]
     x_load = pltpu.make_async_copy(x_hbm, xb, load_sem.at[4, 0])
     x_load.start()
-    for c in loads[0]:
+    for c in loads[0][:2]:
         c.start()
     barrier = pltpu.get_barrier_semaphore()
     for d in range(1, 4):
@@ -131,13 +145,31 @@
             send_sem=send_sem.at[e, g, d - 1], recv_sem=recv_sem.at[e, g, d - 1],
             device_id={'sp': peer}, device_id_type=MESH)
 
-    def spatial(l, e, read_frame, sent, dst):
-        def attention_pair(i, _):
-            rows = attend([read_frame(2 * i + j).astype(F32) for j in range(2)], l, norms, wq, wo, scratch, False)
-            for j in range(2):
-                res[2 * i + j] = rows[j].reshape(4, 4, 16, WIDTH)
-            return 0
-
+    def keep_rows(rows):
+        for f in range(4):
+            res[f] = rows[f].reshape(4, 4, 16, WIDTH)
+
+    def prepare_group(g, _):
+        for d in (1, 2, 3):
+            to_frames(1, sent1, frames2, g, d).wait_recv()
+        x = frames2[:, g].reshape(256, WIDTH).astype(F32)
+        a = layer_norm(x, norms[2, 0:1, :], norms[2, 1:2, :])
+        normed[:, g] = a.reshape(4, 4, 16, WIDTH)
+        qk = dot(a, wq[2, 0:768, :], NT).astype(BF16)
+        queries[:, g] = qk[:, 0:384].reshape(4, 4, 16, WIDTH)
+        keys[:, g] = qk[:, 384:768].reshape(4, 4, 16, WIDTH)
+        return 0
+
+    def attend_prepared(l):
+        xs, values = [], []
+        for f in range(4):
+            frame = lambda ref: ref[:, :, f].reshape(256, WIDTH)
+            xs.append(frame(frames2).astype(F32))
+            values.append(dot(wq[l, 768:1152, :], frame(normed), NT).astype(BF16))
+            head_scores_rows(frame(queries), frame(keys), scratch[0].at[f])
+        keep_rows(attend_end(xs, values, l, wo, scratch, False))
+
+    def spatial_mlp(l, e, sent, dst):
         def mlp_group(g, _):
             rows = jnp.stack([res[:, j, g] for j in range(4)])
             z = mlp(rows.reshape(256, WIDTH), l, norms, wu, wd, hid)
@@ -147,7 +179,6 @@
             dst[g, pl.ds(4 * me, 4)] = sent[g, me]
             return 0
 
-        lax.fori_loop(0, 2, attention_pair, 0)
         lax.fori_loop(0, 4, mlp_group, 0)
 
     def temporal(l, e, src, write):
@@ -180,18 +211,20 @@
             c.wait()
 
     x_load.wait()
-    wait_weights(0)
-    for group in loads[1:]:
-        for c in group:
-            c.start()
-    spatial(0, 0, lambda f: xb[f], sent0, cols1)
+    for c in loads[0][:2]:
+        c.wait()
+    for c in loads[0][2:] + loads[1] + loads[2] + loads[3]:
+        c.start()
+    keep_rows(attend([xb[f].astype(F32) for f in range(4)], 0, norms, wq, wo, scratch, False))
+    for c in loads[0][2:]:
+        c.wait()
+    spatial_mlp(0, 0, sent0, cols1)
     wait_weights(1)
     temporal(1, 0, cols1, send_to_frames)
     wait_weights(2)
-    for g in range(4):
-        for d in (1, 2, 3):
-            to_frames(1, sent1, frames2, g, d).wait_recv()
-    spatial(2, 2, lambda f: frames2[:, :, f].reshape(256, WIDTH), sent2, cols3)
+    lax.fori_loop(0, 4, prepare_group, 0)
+    attend_prepared(2)
+    spatial_mlp(2, 2, sent2, cols3)
     wait_weights(3)
     temporal(3, 2, cols3, write_y)
     for g in range(4):
@@ -223,11 +256,12 @@
                 pltpu.VMEM(groups, BF16), pltpu.VMEM(tokens, BF16),
                 pltpu.VMEM(tokens, BF16), pltpu.VMEM(groups, BF16),
                 pltpu.VMEM(groups, BF16),
+                pltpu.VMEM(tokens, BF16), pltpu.VMEM(tokens, BF16), pltpu.VMEM(tokens, BF16),
                 pltpu.SemaphoreType.DMA((6, 4)),
                 pltpu.SemaphoreType.DMA((3, 4, 3)),
                 pltpu.SemaphoreType.DMA((3, 4, 3)),
-                pltpu.VMEM((2, 6, 256, 256), F32), pltpu.VMEM((2, 6, 256, 256), F32),
-                pltpu.VMEM((2, 6, 256, 256), BF16), pltpu.VMEM((2, WIDTH, 256), BF16),
+                pltpu.VMEM((4, 6, 256, 256), F32), pltpu.VMEM((4, 6, 256, 256), F32),
+                pltpu.VMEM((4, 6, 256, 256), BF16), pltpu.VMEM((4, WIDTH, 256), BF16),
             ],
             compiler_params=pltpu.CompilerParams(collective_id=0, has_side_effects=True, vmem_limit_bytes=56 * 2**20),
         )(latents[0], norms,

time: 53.4 us -> 51.1 us (0.957)
  Pallas kernels: 50.7 us -> 48.7 us
    pallas_call x1, Pallas kernels: 50.7 us -> 48.7 us  [local_stack(): pl.pallas_call(kernel, out_shape=jax.ShapeDtypeStruct((16, 64, WIDTH), BF...]
where the time goes in v4:
time: 51.1 us; the launch traced here: 50.8 us
  Pallas kernels  48.7 us (95%)
  local copies, waits for them, and re-layouts  2.09 us (4%)
    pallas_call x1, Pallas kernels, local_stack(): pl.pallas_call(kernel, out_shape=jax.ShapeDtypeStruct((16, 64, WIDTH), BF...  48.7 us
    unnamed x1, local copies, waits for them, and re-layouts  2.09 us

profile of v4, /device:TPU:0, one launch (start us, length us, event | category | flops | bytes accessed | tf_op | source)
XLA Modules:
  0.0 50.8 jit_solution(523409954268815972)
XLA Ops:
  0.0 48.7 %shard_map.64 = bf16[16,64,384]{2,1,0:T(8,128)(2,1)} custom-call(bf16[4,256,384]{2,1,0:T(8,128)(2,1)} %bitcast.9, f32[4,4,384]{2,1,0:T(4,128)} %norms.1, bf16[4,1152,384]{2,1,0:T(8,128)(2,1)} %bitcast.6, bf16[4,384,384]{2,1,0:T(8,128)(2,1)} %bitcast.8, bf16[4,384,1536]{2,1,0:T(8,128)(2,1)} %wu_hbm.1, bf16[4,1536,384]{2,1,0:T(8,128)(2,1)} %wd_hbm.1), custom_call_target="tpu_custom_call" | custom-call | tf_op jit(solution)/shard_map/pallas_call | solution.py:244
  48.7 2.1 %copy.8 = bf16[1,16,64,384]{3,2,1,0:T(8,128)(2,1)} copy(bf16[1,16,64,384]{3,2,1,0:T(8,128)(2,1)} %bitcast.7) | data formatting | bytes 1572864

commit v5 on v4

--- a/solution.py
+++ b/solution.py
@@ -115,21 +115,22 @@
     return res + dot(hid[...], wd[l], NN)
 
 
-def kernel(x_hbm, norms, wq_hbm, wo_hbm, wu_hbm, wd_hbm, y_hbm,
-           xb, wq, wo, wu, wd, hid, res, sent0, cols1, sent1, frames2, sent2, cols3, yb, normed, queries, keys,
+def kernel(x_hbm, norms_hbm, wq_hbm, wo_hbm, wu_hbm, wd_hbm, y_hbm,
+           xb, norms, wq, wo, wu, wd, hid, res, sent0, cols1, sent1, frames2, sent2, cols3, normed, queries, keys,
            load_sem, send_sem, recv_sem, *scratch):
     me = lax.axis_index('sp')
     pairs = ((wq_hbm, wq), (wo_hbm, wo), (wu_hbm, wu), (wd_hbm, wd))
     loads = [[pltpu.make_async_copy(s.at[l], d.at[l], load_sem.at[l, i]) for i, (s, d) in enumerate(pairs)]
              for l in range(4)]
     x_load = pltpu.make_async_copy(x_hbm, xb, load_sem.at[4, 0])
+    norms_load = pltpu.make_async_copy(norms_hbm, norms, load_sem.at[4, 1])
     x_load.start()
+    norms_load.start()
     for c in loads[0][:2]:
         c.start()
     barrier = pltpu.get_barrier_semaphore()
     for d in range(1, 4):
         pl.semaphore_signal(barrier, inc=1, device_id={'sp': (me + d) % 4}, device_id_type=MESH)
-    pl.semaphore_wait(barrier, 3)
 
     def to_columns(e, src, dst, g, d):
         peer = (me + d) % 4
@@ -198,19 +199,15 @@
             to_frames(1, sent1, frames2, g, d).start()
         frames2[me, g] = sent1[g, pl.ds(4 * me, 4)]
 
-    def y_store(g):
-        return pltpu.make_async_copy(yb.at[g], y_hbm.at[:, pl.ds(pl.multiple_of(16 * g, 16), 16), :],
-                                     load_sem.at[5, g])
-
     def write_y(g, z):
-        yb[g] = z
-        y_store(g).start()
+        y_hbm[:, pl.ds(pl.multiple_of(16 * g, 16), 16), :] = z
 
     def wait_weights(l):
         for c in loads[l]:
             c.wait()
 
     x_load.wait()
+    norms_load.wait()
     for c in loads[0][:2]:
         c.wait()
     for c in loads[0][2:] + loads[1] + loads[2] + loads[3]:
@@ -218,6 +215,7 @@
     keep_rows(attend([xb[f].astype(F32) for f in range(4)], 0, norms, wq, wo, scratch, False))
     for c in loads[0][2:]:
         c.wait()
+    pl.semaphore_wait(barrier, 3)
     spatial_mlp(0, 0, sent0, cols1)
     wait_weights(1)
     temporal(1, 0, cols1, send_to_frames)
@@ -228,7 +226,6 @@
     wait_weights(3)
     temporal(3, 2, cols3, write_y)
     for g in range(4):
-        y_store(g).wait()
         for d in (1, 2, 3):
             to_columns(0, sent0, cols1, g, d).wait_send()
             to_frames(1, sent1, frames2, g, d).wait_send()
@@ -236,7 +233,7 @@
 
 
 def solution(mesh):
-    anyspace = pl.BlockSpec(memory_space=pl.ANY)
+    anyspace = pl.BlockSpec(memory_space=pltpu.HBM)
 
     def local_stack(latents, norms, w_qkv, w_out, w_up, w_down):
         tokens = (4, 4, 4, 16, WIDTH)
@@ -244,10 +241,10 @@
         out = pl.pallas_call(
             kernel,
             out_shape=jax.ShapeDtypeStruct((16, 64, WIDTH), BF16),
-            in_specs=[anyspace, pl.BlockSpec(memory_space=pltpu.VMEM)] + [anyspace] * 4,
-            out_specs=anyspace,
+            in_specs=[anyspace] * 6,
+            out_specs=pl.BlockSpec(memory_space=pltpu.VMEM),
             scratch_shapes=[
-                pltpu.VMEM((4, 256, WIDTH), BF16),
+                pltpu.VMEM((4, 256, WIDTH), BF16), pltpu.VMEM((4, 4, WIDTH), F32),
                 pltpu.VMEM((4, 1152, WIDTH), BF16), pltpu.VMEM((4, WIDTH, WIDTH), BF16),
                 pltpu.VMEM((4, WIDTH, HIDDEN), BF16), pltpu.VMEM((4, HIDDEN, WIDTH), BF16),
                 pltpu.VMEM((256, HIDDEN), BF16),
@@ -255,7 +252,6 @@
                 pltpu.VMEM(tokens, BF16), pltpu.VMEM(groups, BF16),
                 pltpu.VMEM(groups, BF16), pltpu.VMEM(tokens, BF16),
                 pltpu.VMEM(tokens, BF16), pltpu.VMEM(groups, BF16),
-                pltpu.VMEM(groups, BF16),
                 pltpu.VMEM(tokens, BF16), pltpu.VMEM(tokens, BF16), pltpu.VMEM(tokens, BF16),
                 pltpu.SemaphoreType.DMA((6, 4)),
                 pltpu.SemaphoreType.DMA((3, 4, 3)),
@@ -263,10 +259,11 @@
                 pltpu.VMEM((4, 6, 256, 256), F32), pltpu.VMEM((4, 6, 256, 256), F32),
                 pltpu.VMEM((4, 6, 256, 256), BF16), pltpu.VMEM((4, WIDTH, 256), BF16),
             ],
-            compiler_params=pltpu.CompilerParams(collective_id=0, has_side_effects=True, vmem_limit_bytes=56 * 2**20),
-        )(latents[0], norms,
-          w_qkv.transpose(0, 2, 3, 4, 1).reshape(4, 3 * WIDTH, WIDTH),
-          w_out.reshape(4, WIDTH, WIDTH), w_up, w_down)
+            compiler_params=pltpu.CompilerParams(collective_id=0, has_side_effects=True, vmem_limit_bytes=48 * 2**20),
+        )(*[pltpu.with_memory_space_constraint(a, pltpu.HBM) for a in (
+            latents[0], norms,
+            w_qkv.transpose(0, 2, 3, 4, 1).reshape(4, 3 * WIDTH, WIDTH),
+            w_out.reshape(4, WIDTH, WIDTH), w_up, w_down)])
         return out[None]
 
     whole = P()

time: 51.1 us -> 48.6 us (0.951)
  Pallas kernels: 48.7 us -> 47.2 us
  local copies, waits for them, and re-layouts: 2.09 us -> 0.88 us
    pallas_call x1, Pallas kernels: 48.7 us -> 47.2 us  [local_stack(): pl.pallas_call(kernel, out_shape=jax.ShapeDtypeStruct((16, 64, WIDTH), BF...]
    unnamed x1, local copies, waits for them, and re-layouts: 2.09 us -> 0.88 us
where the time goes in v5:
time: 48.6 us; the launch traced here: 48.1 us
  Pallas kernels  47.2 us (97%)
  local copies, waits for them, and re-layouts  0.88 us (2%)
    pallas_call x1, Pallas kernels, local_stack(): pl.pallas_call(kernel, out_shape=jax.ShapeDtypeStruct((16, 64, WIDTH), BF...  47.2 us

profile of v5, /device:TPU:0, one launch (start us, length us, event | category | flops | bytes accessed | tf_op | source)
XLA Modules:
  0.0 48.1 jit_solution(11117297875315871017)
XLA Ops:
  0.0 47.2 %shard_map.64 = bf16[16,64,384]{2,1,0:T(8,128)(2,1)S(1)} custom-call(bf16[4,256,384]{2,1,0:T(8,128)(2,1)} %bitcast.9, f32[4,4,384]{2,1,0:T(4,128)} %norms_hbm.1, bf16[4,1152,384]{2,1,0:T(8,128)(2,1)} %bitcast.7, bf16[4,384,384]{2,1,0:T(8,128)(2,1)} %bitcast.8, bf16[4,384,1536]{2,1,0:T(8,128)(2,1)} %wu_hbm.1, bf16[4,1536,384]{2,1,0:T(8,128)(2,1)} %wd_hbm.1), custom_call_target="tpu_custom_call" | custom-call | tf_op jit(solution)/shard_map/pallas_call | solution.py:241
  47.2 0.9 %copy.8 = bf16[1,16,64,384]{3,2,1,0:T(8,128)(2,1)} copy(bf16[1,16,64,384]{3,2,1,0:T(8,128)(2,1)S(1)} %bitcast.6) | data formatting | bytes 1572864

commit v6 on v5

--- a/solution.py
+++ b/solution.py
@@ -13,6 +13,7 @@
 TN = (((0,), (0,)), ((), ()))
 SCORE_SCALE = 0.125 * 1.4426950408889634
 MESH = pl.DeviceIdType.MESH
+PAIRED, LATE = (3,), ()
 
 
 def dot(a, b, dims):
@@ -78,16 +79,6 @@
             mixed[p + 64:p + 128, t:t + 128] = o[64:128, 128:256]
 
 
-def head_scores_rows(q, k, scores):
-    low = lax.broadcasted_iota(jnp.int32, (256, 128), 1) < 64
-    for h in range(6):
-        p = h // 2 * 128
-        qp = q[:, p:p + 128]
-        zero = jnp.zeros_like(qp)
-        rhs = jnp.where(low, zero, qp) if h % 2 else jnp.where(low, qp, zero)
-        scores[h] = dot(k[:, p:p + 128], rhs, NT)
-
-
 def attend_end(xs, values, l, wo, scratch, temporal):
     for j in range(len(xs)):
         head_probs(scratch[0].at[j], scratch[1].at[j], scratch[2].at[j], temporal)
@@ -116,7 +107,7 @@
 
 
 def kernel(x_hbm, norms_hbm, wq_hbm, wo_hbm, wu_hbm, wd_hbm, y_hbm,
-           xb, norms, wq, wo, wu, wd, hid, res, sent0, cols1, sent1, frames2, sent2, cols3, normed, queries, keys,
+           xb, norms, wq, wo, wu, wd, hid, res, sent0, cols1, sent1, frames2, sent2, cols3, normed, queries, keys, values,
            load_sem, send_sem, recv_sem, *scratch):
     me = lax.axis_index('sp')
     pairs = ((wq_hbm, wq), (wo_hbm, wo), (wu_hbm, wu), (wd_hbm, wd))
@@ -146,9 +137,15 @@
             send_sem=send_sem.at[e, g, d - 1], recv_sem=recv_sem.at[e, g, d - 1],
             device_id={'sp': peer}, device_id_type=MESH)
 
-    def keep_rows(rows):
+    def keep_queries(qk, at):
+        queries[at] = qk[:, 0:384].astype(BF16).reshape(4, 4, 16, WIDTH)
+        keys[at] = qk[:, 384:768].astype(BF16).reshape(4, 4, 16, WIDTH)
+
+    def prepare_frames():
         for f in range(4):
-            res[f] = rows[f].reshape(4, 4, 16, WIDTH)
+            a = layer_norm(xb[f].reshape(256, WIDTH).astype(F32), norms[0, 0:1, :], norms[0, 1:2, :])
+            keep_queries(dot(a, wq[0, 0:768, :], NT), (slice(None), slice(None), f))
+            values[f] = dot(wq[0, 768:1152, :], a, NT).astype(BF16)
 
     def prepare_group(g, _):
         for d in (1, 2, 3):
@@ -156,42 +153,83 @@
         x = frames2[:, g].reshape(256, WIDTH).astype(F32)
         a = layer_norm(x, norms[2, 0:1, :], norms[2, 1:2, :])
         normed[:, g] = a.reshape(4, 4, 16, WIDTH)
-        qk = dot(a, wq[2, 0:768, :], NT).astype(BF16)
-        queries[:, g] = qk[:, 0:384].reshape(4, 4, 16, WIDTH)
-        keys[:, g] = qk[:, 384:768].reshape(4, 4, 16, WIDTH)
+        keep_queries(dot(a, wq[2, 0:768, :], NT), (slice(None), g))
         return 0
 
-    def attend_prepared(l):
-        xs, values = [], []
+    def prepare_values():
         for f in range(4):
-            frame = lambda ref: ref[:, :, f].reshape(256, WIDTH)
-            xs.append(frame(frames2).astype(F32))
-            values.append(dot(wq[l, 768:1152, :], frame(normed), NT).astype(BF16))
-            head_scores_rows(frame(queries), frame(keys), scratch[0].at[f])
-        keep_rows(attend_end(xs, values, l, wo, scratch, False))
-
-    def spatial_mlp(l, e, sent, dst):
-        def mlp_group(g, _):
-            rows = jnp.stack([res[:, j, g] for j in range(4)])
-            z = mlp(rows.reshape(256, WIDTH), l, norms, wu, wd, hid)
-            sent[g] = z.astype(BF16).reshape(4, 4, 16, WIDTH)
-            for d in (2, 1, 3):
-                to_columns(e, sent, dst, g, d).start()
-            dst[g, pl.ds(4 * me, 4)] = sent[g, me]
+            values[f] = dot(wq[2, 768:1152, :], normed[:, :, f].reshape(256, WIDTH), NT).astype(BF16)
+
+    def attend_half(l, half, read):
+        scores, expd, probs, mixed = scratch
+        groups = pl.ds(2 * half, 2)
+        low = lax.broadcasted_iota(jnp.int32, (128, 128), 1) < 64
+        for f in range(4):
+            q = queries[:, groups, f].reshape(128, WIDTH)
+            k = keys[:, :, f].reshape(256, WIDTH)
+            for p in range(3):
+                qp = q[:, 128 * p:128 * p + 128]
+                zero = jnp.zeros_like(qp)
+                rhs = jnp.concatenate([jnp.where(low, qp, zero), jnp.where(low, zero, qp)], 0)
+                scores[f // 2, 3 * (f % 2) + p] = dot(k[:, 128 * p:128 * p + 128], rhs, NT)
+        for j in range(2):
+            head_probs(scores.at[j], expd.at[j], probs.at[j], False)
+        for f in range(4):
+            lanes = 128 * (f % 2)
+            for p in range(3):
+                r = 128 * p
+                o = dot(values[f, r:r + 128, :], probs[f // 2, 3 * (f % 2) + p], NN).astype(BF16)
+                mixed[f // 2, r:r + 64, lanes:lanes + 128] = o[0:64, 0:128]
+                mixed[f // 2, r + 64:r + 128, lanes:lanes + 128] = o[64:128, 128:256]
+        for j in range(2):
+            x = jnp.concatenate([read(2 * j + u, groups).reshape(128, WIDTH) for u in range(2)], 0)
+            rows = (x.astype(F32) + dot(mixed[j], wo[l], TN)).astype(BF16)
+            for u in range(2):
+                res[2 * j + u, :, groups] = rows[128 * u:128 * u + 128].reshape(4, 2, 16, WIDTH)
+
+    def spatial_rest(l, e, read, sent, dst, before_send):
+        def half_step(half, _):
+            attend_half(l, half, read)
+            def group_mlp(u):
+                rows = jnp.stack([res[:, j, 2 * half + u] for j in range(4)])
+                z = mlp(rows.reshape(256, WIDTH), l, norms, wu, wd, hid.at[u])
+                sent[2 * half + u] = z.astype(BF16).reshape(4, 4, 16, WIDTH)
+
+            def send(u):
+                g = 2 * half + u
+                for d in (2, 1, 3):
+                    to_columns(e, sent, dst, g, d).start()
+                dst[g, pl.ds(4 * me, 4)] = sent[g, me]
+
+            if l in LATE:
+                for u in range(2):
+                    group_mlp(u)
+                for u in range(2):
+                    send(u)
+            else:
+                for u in range(2):
+                    group_mlp(u)
+                    send(u)
             return 0
-
-        lax.fori_loop(0, 4, mlp_group, 0)
+        before_send()
+        lax.fori_loop(0, 2, half_step, 0)
 
     def temporal(l, e, src, write):
-        def body(g, _):
-            for d in (1, 2, 3):
-                to_columns(e, sent0, src, g, d).wait_recv()
-            x = swap_halves(src[g].reshape(256, WIDTH).astype(F32), 16, 2)
-            rows = attend([x], l, norms, wq, wo, scratch, True)
-            z = mlp(rows[0], l, norms, wu, wd, hid)
-            write(g, swap_halves(z, 2, 16).astype(BF16).reshape(16, 16, WIDTH))
+        n = 2 if l in PAIRED else 1
+
+        def body(i, _):
+            xs = []
+            for j in range(n):
+                for d in (1, 2, 3):
+                    to_columns(e, sent0, src, n * i + j, d).wait_recv()
+            for j in range(n):
+                xs.append(swap_halves(src[n * i + j].reshape(256, WIDTH).astype(F32), 16, 2))
+            rows = attend(xs, l, norms, wq, wo, scratch, True)
+            zs = [mlp(rows[j], l, norms, wu, wd, hid.at[j]) for j in range(n)]
+            for j in range(n):
+                write(n * i + j, swap_halves(zs[j], 2, 16).astype(BF16).reshape(16, 16, WIDTH))
             return 0
-        lax.fori_loop(0, 4, body, 0)
+        lax.fori_loop(0, 4 // n, body, 0)
 
     def send_to_frames(g, z):
         sent1[g] = z
@@ -212,17 +250,20 @@
         c.wait()
     for c in loads[0][2:] + loads[1] + loads[2] + loads[3]:
         c.start()
-    keep_rows(attend([xb[f].astype(F32) for f in range(4)], 0, norms, wq, wo, scratch, False))
-    for c in loads[0][2:]:
-        c.wait()
-    pl.semaphore_wait(barrier, 3)
-    spatial_mlp(0, 0, sent0, cols1)
+    prepare_frames()
+
+    def block0_ready():
+        for c in loads[0][2:]:
+            c.wait()
+        pl.semaphore_wait(barrier, 3)
+
+    spatial_rest(0, 0, lambda f, groups: xb[f, :, groups], sent0, cols1, block0_ready)
     wait_weights(1)
     temporal(1, 0, cols1, send_to_frames)
     wait_weights(2)
     lax.fori_loop(0, 4, prepare_group, 0)
-    attend_prepared(2)
-    spatial_mlp(2, 2, sent2, cols3)
+    prepare_values()
+    spatial_rest(2, 2, lambda f, groups: frames2[:, groups, f], sent2, cols3, lambda: None)
     wait_weights(3)
     temporal(3, 2, cols3, write_y)
     for g in range(4):
@@ -244,24 +285,25 @@
             in_specs=[anyspace] * 6,
             out_specs=pl.BlockSpec(memory_space=pltpu.VMEM),
             scratch_shapes=[
-                pltpu.VMEM((4, 256, WIDTH), BF16), pltpu.VMEM((4, 4, WIDTH), F32),
+                pltpu.VMEM(tokens, BF16), pltpu.VMEM((4, 4, WIDTH), F32),
                 pltpu.VMEM((4, 1152, WIDTH), BF16), pltpu.VMEM((4, WIDTH, WIDTH), BF16),
                 pltpu.VMEM((4, WIDTH, HIDDEN), BF16), pltpu.VMEM((4, HIDDEN, WIDTH), BF16),
-                pltpu.VMEM((256, HIDDEN), BF16),
+                pltpu.VMEM((2, 256, HIDDEN), BF16),
                 pltpu.VMEM(tokens, BF16),
                 pltpu.VMEM(tokens, BF16), pltpu.VMEM(groups, BF16),
                 pltpu.VMEM(groups, BF16), pltpu.VMEM(tokens, BF16),
                 pltpu.VMEM(tokens, BF16), pltpu.VMEM(groups, BF16),
                 pltpu.VMEM(tokens, BF16), pltpu.VMEM(tokens, BF16), pltpu.VMEM(tokens, BF16),
+                pltpu.VMEM((4, WIDTH, 256), BF16),
                 pltpu.SemaphoreType.DMA((6, 4)),
                 pltpu.SemaphoreType.DMA((3, 4, 3)),
                 pltpu.SemaphoreType.DMA((3, 4, 3)),
-                pltpu.VMEM((4, 6, 256, 256), F32), pltpu.VMEM((4, 6, 256, 256), F32),
-                pltpu.VMEM((4, 6, 256, 256), BF16), pltpu.VMEM((4, WIDTH, 256), BF16),
+                pltpu.VMEM((2, 6, 256, 256), F32), pltpu.VMEM((2, 6, 256, 256), F32),
+                pltpu.VMEM((2, 6, 256, 256), BF16), pltpu.VMEM((2, WIDTH, 256), BF16),
             ],
             compiler_params=pltpu.CompilerParams(collective_id=0, has_side_effects=True, vmem_limit_bytes=48 * 2**20),
         )(*[pltpu.with_memory_space_constraint(a, pltpu.HBM) for a in (
-            latents[0], norms,
+            latents.reshape(tokens), norms,
             w_qkv.transpose(0, 2, 3, 4, 1).reshape(4, 3 * WIDTH, WIDTH),
             w_out.reshape(4, WIDTH, WIDTH), w_up, w_down)])
         return out[None]

time: 48.6 us -> 46.7 us (0.961)
  Pallas kernels: 47.2 us -> 45.7 us
    pallas_call x1, Pallas kernels: 47.2 us -> 45.7 us  [local_stack(): pl.pallas_call(kernel, out_shape=jax.ShapeDtypeStruct((16, 64, WIDTH), BF...]
where the time goes in v6:
time: 46.7 us; the launch traced here: 46.6 us
  Pallas kernels  45.7 us (98%)
  local copies, waits for them, and re-layouts  0.88 us (2%)
    pallas_call x1, Pallas kernels, local_stack(): pl.pallas_call(kernel, out_shape=jax.ShapeDtypeStruct((16, 64, WIDTH), BF...  45.7 us

profile of v6, /device:TPU:0, one launch (start us, length us, event | category | flops | bytes accessed | tf_op | source)
XLA Modules:
  0.0 46.6 jit_solution(13704433546969183324)
XLA Ops:
  0.0 45.7 %shard_map.64 = bf16[16,64,384]{2,1,0:T(8,128)(2,1)S(1)} custom-call(bf16[4,4,4,16,384]{4,3,2,1,0:T(8,128)(2,1)} %bitcast.9, f32[4,4,384]{2,1,0:T(4,128)} %norms_hbm.1, bf16[4,1152,384]{2,1,0:T(8,128)(2,1)} %bitcast.7, bf16[4,384,384]{2,1,0:T(8,128)(2,1)} %bitcast.8, bf16[4,384,1536]{2,1,0:T(8,128)(2,1)} %wu_hbm.1, bf16[4,1536,384]{2,1,0:T(8,128)(2,1)} %wd_hbm.1), custom_call_target="tpu_custom_call" | custom-call | tf_op jit(solution)/shard_map/pallas_call | solution.py:282
  45.7 0.9 %copy.8 = bf16[1,16,64,384]{3,2,1,0:T(8,128)(2,1)} copy(bf16[1,16,64,384]{3,2,1,0:T(8,128)(2,1)S(1)} %bitcast.6) | data formatting | bytes 1572864

commit v7 on v6

--- a/solution.py
+++ b/solution.py
@@ -26,10 +26,9 @@
     return (centered * lax.rsqrt(variance + EPS) * gain + shift).astype(BF16)
 
 
-def gelu(x):
+def gelu_of_half(h):
     c = 0.7978845608028654
-    half = 0.5 * x
-    return (half + half * jnp.tanh(x * (c + (c * 0.044715) * (x * x)))).astype(BF16)
+    return (h + h * jnp.tanh(h * (2.0 * c + (8.0 * c * 0.044715) * (h * h)))).astype(BF16)
 
 
 def swap_halves(x, a, b):
@@ -100,9 +99,9 @@
 
 def mlp(res, l, norms, wu, wd, hid):
     res = res.astype(F32)
-    a = layer_norm(res, norms[l, 2:3, :], norms[l, 3:4, :])
+    half = layer_norm(res, 0.5 * norms[l, 2:3, :], 0.5 * norms[l, 3:4, :])
     for c in range(0, HIDDEN, 512):
-        hid[:, c:c + 512] = gelu(dot(a, wu[l, :, c:c + 512], NN))
+        hid[:, c:c + 512] = gelu_of_half(dot(half, wu[l, :, c:c + 512], NN))
     return res + dot(hid[...], wd[l], NN)
 
 

time: 46.7 us -> 45.4 us (0.972)
  Pallas kernels: 45.7 us -> 44.4 us
    pallas_call x1, Pallas kernels: 45.7 us -> 44.4 us  [local_stack(): pl.pallas_call(kernel, out_shape=jax.ShapeDtypeStruct((16, 64, WIDTH), BF...]
where the time goes in v7:
time: 45.4 us; the launch traced here: 45.3 us
  Pallas kernels  44.4 us (98%)
  local copies, waits for them, and re-layouts  0.88 us (2%)
    pallas_call x1, Pallas kernels, local_stack(): pl.pallas_call(kernel, out_shape=jax.ShapeDtypeStruct((16, 64, WIDTH), BF...  44.4 us

profile of v7, /device:TPU:0, one launch (start us, length us, event | category | flops | bytes accessed | tf_op | source)
XLA Modules:
  0.0 45.3 jit_solution(4573789013673737461)
XLA Ops:
  0.0 44.4 %shard_map.64 = bf16[16,64,384]{2,1,0:T(8,128)(2,1)S(1)} custom-call(bf16[4,4,4,16,384]{4,3,2,1,0:T(8,128)(2,1)} %bitcast.9, f32[4,4,384]{2,1,0:T(4,128)} %norms_hbm.1, bf16[4,1152,384]{2,1,0:T(8,128)(2,1)} %bitcast.7, bf16[4,384,384]{2,1,0:T(8,128)(2,1)} %bitcast.8, bf16[4,384,1536]{2,1,0:T(8,128)(2,1)} %wu_hbm.1, bf16[4,1536,384]{2,1,0:T(8,128)(2,1)} %wd_hbm.1), custom_call_target="tpu_custom_call" | custom-call | tf_op jit(solution)/shard_map/pallas_call | solution.py:281
  44.4 0.9 %copy.8 = bf16[1,16,64,384]{3,2,1,0:T(8,128)(2,1)} copy(bf16[1,16,64,384]{3,2,1,0:T(8,128)(2,1)S(1)} %bitcast.6) | data formatting | bytes 1572864

commit v8 on v7

--- a/solution.py
+++ b/solution.py
@@ -106,7 +106,7 @@
 
 
 def kernel(x_hbm, norms_hbm, wq_hbm, wo_hbm, wu_hbm, wd_hbm, y_hbm,
-           xb, norms, wq, wo, wu, wd, hid, res, sent0, cols1, sent1, frames2, sent2, cols3, normed, queries, keys, values,
+           xb, norms, wq, wo, wu, wd, hid, res, sent0, cols1, sent1, frames2, sent2, cols3, value_rows, queries, keys, values,
            load_sem, send_sem, recv_sem, *scratch):
     me = lax.axis_index('sp')
     pairs = ((wq_hbm, wq), (wo_hbm, wo), (wu_hbm, wu), (wd_hbm, wd))
@@ -151,13 +151,14 @@
             to_frames(1, sent1, frames2, g, d).wait_recv()
         x = frames2[:, g].reshape(256, WIDTH).astype(F32)
         a = layer_norm(x, norms[2, 0:1, :], norms[2, 1:2, :])
-        normed[:, g] = a.reshape(4, 4, 16, WIDTH)
-        keep_queries(dot(a, wq[2, 0:768, :], NT), (slice(None), g))
+        qkv = dot(a, wq[2], NT)
+        keep_queries(qkv, (slice(None), g))
+        value_rows[:, g] = qkv[:, 768:1152].astype(BF16).reshape(4, 4, 16, WIDTH)
         return 0
 
     def prepare_values():
         for f in range(4):
-            values[f] = dot(wq[2, 768:1152, :], normed[:, :, f].reshape(256, WIDTH), NT).astype(BF16)
+            values[f] = value_rows[:, :, f].reshape(256, WIDTH).T
 
     def attend_half(l, half, read):
         scores, expd, probs, mixed = scratch
@@ -247,13 +248,15 @@
     norms_load.wait()
     for c in loads[0][:2]:
         c.wait()
-    for c in loads[0][2:] + loads[1] + loads[2] + loads[3]:
+    for c in loads[0][2:]:
         c.start()
     prepare_frames()
 
     def block0_ready():
         for c in loads[0][2:]:
             c.wait()
+        for c in loads[1] + loads[2] + loads[3]:
+            c.start()
         pl.semaphore_wait(barrier, 3)
 
     spatial_rest(0, 0, lambda f, groups: xb[f, :, groups], sent0, cols1, block0_ready)

time: 45.4 us -> 45.2 us (level)
  no operation moved by 1% of the time
where the time goes in v8:
time: 45.2 us; the launch traced here: 45.1 us
  Pallas kernels  44.2 us (98%)
  local copies, waits for them, and re-layouts  0.88 us (2%)
    pallas_call x1, Pallas kernels, local_stack(): pl.pallas_call(kernel, out_shape=jax.ShapeDtypeStruct((16, 64, WIDTH), BF...  44.2 us

profile of v8, /device:TPU:0, one launch (start us, length us, event | category | flops | bytes accessed | tf_op | source)
XLA Modules:
  0.0 45.1 jit_solution(11911946253518818549)
XLA Ops:
  0.0 44.2 %shard_map.64 = bf16[16,64,384]{2,1,0:T(8,128)(2,1)S(1)} custom-call(bf16[4,4,4,16,384]{4,3,2,1,0:T(8,128)(2,1)} %bitcast.9, f32[4,4,384]{2,1,0:T(4,128)} %norms_hbm.1, bf16[4,1152,384]{2,1,0:T(8,128)(2,1)} %bitcast.7, bf16[4,384,384]{2,1,0:T(8,128)(2,1)} %bitcast.8, bf16[4,384,1536]{2,1,0:T(8,128)(2,1)} %wu_hbm.1, bf16[4,1536,384]{2,1,0:T(8,128)(2,1)} %wd_hbm.1), custom_call_target="tpu_custom_call" | custom-call | tf_op jit(solution)/shard_map/pallas_call | solution.py:284
  44.2 0.9 %copy.8 = bf16[1,16,64,384]{3,2,1,0:T(8,128)(2,1)} copy(bf16[1,16,64,384]{3,2,1,0:T(8,128)(2,1)S(1)} %bitcast.6) | data formatting | bytes 1572864

commit v9 on v8

--- a/solution.py
+++ b/solution.py
@@ -116,8 +116,7 @@
     norms_load = pltpu.make_async_copy(norms_hbm, norms, load_sem.at[4, 1])
     x_load.start()
     norms_load.start()
-    for c in loads[0][:2]:
-        c.start()
+    loads[0][0].start()
     barrier = pltpu.get_barrier_semaphore()
     for d in range(1, 4):
         pl.semaphore_signal(barrier, inc=1, device_id={'sp': (me + d) % 4}, device_id_type=MESH)
@@ -246,14 +245,13 @@
 
     x_load.wait()
     norms_load.wait()
-    for c in loads[0][:2]:
-        c.wait()
-    for c in loads[0][2:]:
+    loads[0][0].wait()
+    for c in loads[0][1:]:
         c.start()
     prepare_frames()
 
     def block0_ready():
-        for c in loads[0][2:]:
+        for c in loads[0][1:]:
             c.wait()
         for c in loads[1] + loads[2] + loads[3]:
             c.start()

time: 45.2 us -> 45.3 us (level)
  no operation moved by 1% of the time
where the time goes in v9:
time: 45.3 us; the launch traced here: 45.1 us
  Pallas kernels  44.2 us (98%)
  local copies, waits for them, and re-layouts  0.88 us (2%)
    pallas_call x1, Pallas kernels, local_stack(): pl.pallas_call(kernel, out_shape=jax.ShapeDtypeStruct((16, 64, WIDTH), BF...  44.2 us

profile of v9, /device:TPU:0, one launch (start us, length us, event | category | flops | bytes accessed | tf_op | source)
XLA Modules:
  0.0 45.1 jit_solution(6525609312296677760)
XLA Ops:
  0.0 44.2 %shard_map.64 = bf16[16,64,384]{2,1,0:T(8,128)(2,1)S(1)} custom-call(bf16[4,4,4,16,384]{4,3,2,1,0:T(8,128)(2,1)} %bitcast.9, f32[4,4,384]{2,1,0:T(4,128)} %norms_hbm.1, bf16[4,1152,384]{2,1,0:T(8,128)(2,1)} %bitcast.7, bf16[4,384,384]{2,1,0:T(8,128)(2,1)} %bitcast.8, bf16[4,384,1536]{2,1,0:T(8,128)(2,1)} %wu_hbm.1, bf16[4,1536,384]{2,1,0:T(8,128)(2,1)} %wd_hbm.1), custom_call_target="tpu_custom_call" | custom-call | tf_op jit(solution)/shard_map/pallas_call | solution.py:282
  44.2 0.9 %copy.8 = bf16[1,16,64,384]{3,2,1,0:T(8,128)(2,1)} copy(bf16[1,16,64,384]{3,2,1,0:T(8,128)(2,1)S(1)} %bitcast.6) | data formatting | bytes 1572864
